TPU v7x, 32 devices: a whole 2x2x4 slice. The times are simulated.
32 devices in a mesh: dp: 8 (over y, x, core), tensor: 4 (over z).
Axes of the slice: x: 2, y: 2, z: 4, core: 2. Of those that a mesh axis runs over, the one named last changes fastest.
Arguments:
- activations: bfloat16 [3072, 16384], P(('dp', 'tensor')), may hold values from -6 to 6
- out_grad: bfloat16 [3072, 16384], P('dp', 'tensor'), may hold values from -0.25 to 0.25
- block_ids: int32 [4, 12], replicated, may hold values from 0 to 127, as said below
- owner_map: int32 [8, 4], replicated, may hold values from 0 to 1, as said below
- master: float32 [1024, 16384], P('dp', 'tensor'), may hold values from -3 to 3
- moment: float32 [1024, 16384], P('dp', 'tensor'), may hold values from -3 to 3
- second: float32 [1024, 16384], P('dp', 'tensor'), may hold values from 0.01 to 2
Outputs:
- new_master: float32 [1024, 16384], P('dp', 'tensor')
- new_moment: float32 [1024, 16384], P('dp', 'tensor')
- new_second: float32 [1024, 16384], P('dp', 'tensor')
- hot_weights: bfloat16 [1024, 16384], P('dp')
- cold_recv: float32 [4096, 16384], P('dp', 'tensor')
Inputs may be any that keep to these rules, and one draw needn't show every extreme that they name: `block_ids`: the 12 block numbers in a row are distinct. `owner_map`: each row has between 1 and 3 ones; some row has exactly 3 ones and some row exactly 1.
All inputs are finite; a program needn't handle non-finite values.
Results may differ from a plain program's by a relative error of at most 0.006.
Values may be sent and summed in bfloat16 or wider, within the bound.
A program may use at most 128 MiB of HBM per device.

v0:
```python
import functools

import jax
import jax.numpy as jnp
from jax import lax
from jax.experimental import pallas as pl
from jax.experimental.pallas import tpu as pltpu
from jax.sharding import PartitionSpec as P

BLOCK = 128
HOT = 8
COLD = 4
MOSTC = 3

BETA_ONE = 0.9
BETA_TWO = 0.95
ADAM_EPS = 1e-08
LEARN_RATE = 0.01
DECAY = 0.1
CORRECT_ONE = 1.0 - 0.9**10
CORRECT_TWO = 1.0 - 0.95**10

CHUNKS = 8
MESH = pl.DeviceIdType.MESH
F32 = jnp.float32
BF16 = jnp.bfloat16


def adam(grad, master, moment, second):
    new_moment = BETA_ONE * moment + (1.0 - BETA_ONE) * grad
    new_second = BETA_TWO * second + (1.0 - BETA_TWO) * grad * grad
    update = new_moment / CORRECT_ONE / (jnp.sqrt(new_second / CORRECT_TWO) + ADAM_EPS)
    return master - LEARN_RATE * (update + DECAY * master), new_moment, new_second


def halvings(n_dp):
    bits = []
    bit = n_dp // 2
    while bit >= 2:
        bits.append(bit)
        bit //= 2
    return bits


def flip(d, bit):
    return d + bit - 2 * bit * ((d // bit) % 2)


def gather_kernel(n_dp, n_t, unit, ids_ref, owner_ref, act, outbox, cold_outbox):
    i = lax.axis_index("dp")
    t = lax.axis_index("tensor")
    peer = flip(i, 1)
    bits = halvings(n_dp)
    half = outbox.shape[4] // unit

    owned = [owner_ref[i, c] for c in range(COLD)]
    ones = owned[0]
    for c in range(1, COLD):
        ones = ones + owned[c]
    place, taken, left = [], 0, ones
    for c in range(COLD):
        place.append(jnp.where(owned[c] == 1, taken, left))
        taken, left = taken + owned[c], left + 1 - owned[c]

    def column(block):
        return act[:, pl.ds(pl.multiple_of(block * BLOCK, BLOCK), BLOCK)]

    def hot_unit(group, d):
        index = (d * unit) // BLOCK
        cols = column(ids_ref[group, index])
        if unit < BLOCK:
            share = BLOCK // unit
            picked = cols[:, :unit]
            for s in range(1, share):
                picked = jnp.where(d % share == s, cols[:, s * unit : (s + 1) * unit], picked)
            cols = picked
        return cols

    for who, base in ((0, i), (1, peer)):
        for part in range(2):
            for k in range(n_t):
                group = (t + k) % n_t
                for u in range(half):
                    r = 2 * (u + half * (1 - part))
                    d = base
                    for b in bits:
                        if r & b:
                            d = flip(d, b)
                    cols = hot_unit(group, d)
                    outbox[who, part, k, :, pl.ds(u * unit, unit)] = cols
    for k in range(n_t):
        group = (t + k) % n_t
        for p in range(COLD):
            block = 0
            for c in range(COLD):
                block = block + jnp.where(place[c] == p, ids_ref[group, HOT + c], 0)
            cold_outbox[k, :, pl.ds(p * BLOCK, BLOCK)] = column(block)


def gather(n_dp, n_t, unit, ids, owner_map, activations):
    rows_tok = activations.shape[0]
    half = max(n_dp // 4, 1)
    smem = pl.BlockSpec(memory_space=pltpu.SMEM)
    vmem = pl.BlockSpec(memory_space=pltpu.VMEM)
    return pl.pallas_call(
        functools.partial(gather_kernel, n_dp, n_t, unit),
        out_shape=(
            jax.ShapeDtypeStruct((2, 2, n_t, rows_tok, half * unit), BF16),
            jax.ShapeDtypeStruct((n_t, rows_tok, COLD * BLOCK), BF16),
        ),
        in_specs=[smem, smem, vmem],
        out_specs=[vmem, vmem],
    )(ids, owner_map, activations)


def exchange_kernel(
    n_dp,
    n_t,
    outbox,
    cold_outbox,
    og_hbm,
    master_hbm,
    moment_hbm,
    second_hbm,
    grad_out,
    hot_out,
    prev_out,
    next_out,
    inbox,
    cold_inbox,
    og,
    lhs,
    cold_lhs,
    acc,
    rs_send,
    rs_recv,
    cold_send,
    master,
    moment,
    second,
    grad,
    hot_send,
    load_sem,
    sel_send_sem,
    sel_recv_sem,
    og_send_sem,
    og_recv_sem,
    rs_send_sem,
    rs_recv_sem,
    cold_send_sem,
    cold_recv_sem,
    hot_send_sem,
    hot_recv_sem,
    out_sem,
):
    i = lax.axis_index("dp")
    t = lax.axis_index("tensor")
    peer = flip(i, 1)
    rows_tok = cold_outbox.shape[1]
    tok, qlocal = og.shape[0] // 2, og.shape[1]
    units = n_dp // 2
    unit = grad.shape[0]
    half = max(units // 2, 1)
    hw = half * unit
    chunk = qlocal // CHUNKS

    loads = [
        pltpu.make_async_copy(og_hbm, og.at[pl.ds(0, tok)], load_sem.at[0]),
        pltpu.make_async_copy(master_hbm, master, load_sem.at[1]),
        pltpu.make_async_copy(moment_hbm, moment, load_sem.at[2]),
        pltpu.make_async_copy(second_hbm, second, load_sem.at[3]),
    ]
    loads[0].start()

    bits = halvings(n_dp)
    nxt, prv = (i + 1) % n_dp, (i + n_dp - 1) % n_dp
    partners = [(flip(i, b), t) for b in bits] + [(nxt, t), (prv, t), (peer, t)]
    for k in range(1, n_t):
        partners += [(i, (t + k) % n_t), (peer, (t + k) % n_t)]
    barrier = pltpu.get_barrier_semaphore()
    for partner in partners:
        pl.semaphore_signal(barrier, inc=1, device_id=partner, device_id_type=MESH)

    mine = pl.ds(t * rows_tok, rows_tok)
    for part in range(2):
        inbox[part, 0, mine, :] = outbox[0, part, 0]
    cold_inbox[mine, :] = cold_outbox[0]

    pl.semaphore_wait(barrier, len(partners))

    def sel_copy(who, part, k):
        return pltpu.make_async_remote_copy(
            src_ref=outbox.at[who, part, k],
            dst_ref=inbox.at[part, who, pl.ds(t * rows_tok, rows_tok)],
            send_sem=sel_send_sem.at[who, part, k],
            recv_sem=sel_recv_sem.at[who, part, k],
            device_id=(i if who == 0 else peer, (t + k) % n_t),
            device_id_type=MESH,
        )

    def cold_sel_copy(k):
        return pltpu.make_async_remote_copy(
            src_ref=cold_outbox.at[k],
            dst_ref=cold_inbox.at[pl.ds(t * rows_tok, rows_tok)],
            send_sem=sel_send_sem.at[0, 2, k],
            recv_sem=sel_recv_sem.at[0, 2, k],
            device_id=(i, (t + k) % n_t),
            device_id_type=MESH,
        )

    sel = {0: [], 1: [], 2: []}
    for part in range(2):
        for k in range(n_t):
            for who in range(2):
                if who or k:
                    sel[part].append(sel_copy(who, part, k))
    for k in range(1, n_t):
        sel[2].append(cold_sel_copy(k))
    og_copy = pltpu.make_async_remote_copy(
        src_ref=og_hbm,
        dst_ref=og.at[pl.ds(tok, tok)],
        send_sem=og_send_sem,
        recv_sem=og_recv_sem,
        device_id=(peer, t),
        device_id_type=MESH,
    )
    for copy in sel[0]:
        copy.start()
    og_copy.start()
    for load in loads[1:]:
        load.start()

    counts = [b // 2 for b in bits]
    offset = [sum(counts[:s]) * unit for s in range(len(bits))]

    def rs_copy(s, q):
        place_ = (pl.ds(offset[s], counts[s] * unit), pl.ds(q * chunk, chunk))
        return pltpu.make_async_remote_copy(
            src_ref=rs_send.at[place_],
            dst_ref=rs_recv.at[place_],
            send_sem=rs_send_sem.at[s, q],
            recv_sem=rs_recv_sem.at[s, q],
            device_id=(flip(i, bits[s]), t),
            device_id_type=MESH,
        )

    tile = min(512, chunk)

    def product(lhs_value_ref, rows, depth, col):
        return jnp.dot(
            lhs_value_ref[rows, :],
            og[pl.ds(0, depth), pl.ds(col, tile)],
            preferred_element_type=F32,
        )

    def wait_sel(part):
        for copy in sel[part]:
            copy.wait_recv()

    wait_sel(0)
    for part in (2, 1):
        for copy in sel[part]:
            copy.start()
    lhs[0, :, pl.ds(0, tok)] = inbox[0, 0].T
    lhs[0, :, pl.ds(tok, tok)] = inbox[0, 1].T
    loads[0].wait()
    og_copy.wait_recv()
    for q in range(CHUNKS):

        @pl.loop(0, chunk // tile)
        def _(n):
            col = pl.multiple_of(q * chunk + n * tile, tile)
            rs_send[pl.ds(0, hw), pl.ds(col, tile)] = product(
                lhs.at[0], slice(None), 2 * tok, col
            ).astype(BF16)

        rs_copy(0, q).start()

    def cold_copy(p, ahead, q):
        slot = p if ahead else p - 1
        place_ = (slot, slice(None), pl.ds(q * chunk, chunk))
        which = 0 if ahead else 1
        return pltpu.make_async_remote_copy(
            src_ref=cold_send.at[p, :, pl.ds(q * chunk, chunk)],
            dst_ref=(prev_out if ahead else next_out).at[place_],
            send_sem=cold_send_sem.at[which, slot, q],
            recv_sem=cold_recv_sem.at[which, slot, q],
            device_id=(nxt if ahead else prv, t),
            device_id_type=MESH,
        )

    wait_sel(2)
    cold_lhs[...] = cold_inbox[...].T
    for q in range(CHUNKS):

        @pl.loop(0, chunk // tile)
        def _(n):
            col = pl.multiple_of(q * chunk + n * tile, tile)
            out = product(cold_lhs, slice(None), tok, col).astype(BF16)
            for p in range(COLD):
                cold_send[p, :, pl.ds(col, tile)] = out[p * BLOCK : (p + 1) * BLOCK]

    def send_cold(q):
        for slot in range(MOSTC):
            cold_copy(slot, True, q).start()
            cold_copy(slot + COLD - MOSTC, False, q).start()

    wait_sel(1)
    lhs[1, :, pl.ds(0, tok)] = inbox[1, 0].T
    lhs[1, :, pl.ds(tok, tok)] = inbox[1, 1].T

    @pl.loop(0, qlocal // tile)
    def _(n):
        col = pl.multiple_of(n * tile, tile)
        acc[:, pl.ds(col, tile)] = product(lhs.at[1], slice(None), 2 * tok, col)

    for load in loads[1:]:
        load.wait()

    def hot_copy(k, q):
        return pltpu.make_async_remote_copy(
            src_ref=hot_send.at[:, pl.ds(q * chunk, chunk)],
            dst_ref=hot_out.at[:, pl.ds(t * qlocal + q * chunk, chunk)],
            send_sem=hot_send_sem.at[k, q],
            recv_sem=hot_recv_sem.at[k, q],
            device_id=(i, (t + k) % n_t),
            device_id_type=MESH,
        )

    def grad_store(q):
        cols = pl.ds(q * chunk, chunk)
        return pltpu.make_async_copy(grad.at[:, cols], grad_out.at[:, cols], out_sem.at[0, q])

    def hot_store(q):
        return pltpu.make_async_copy(
            hot_send.at[:, pl.ds(q * chunk, chunk)],
            hot_out.at[:, pl.ds(t * qlocal + q * chunk, chunk)],
            out_sem.at[1, q],
        )

    step = min(256, chunk)

    def settle(s, q):
        rs_copy(s, q).wait_recv()
        last = s == len(bits) - 1

        @pl.loop(0, chunk // step)
        def _(n):
            cols = pl.ds(pl.multiple_of(q * chunk + n * step, step), step)
            keep = counts[s] * unit
            got = rs_recv[pl.ds(offset[s], keep), cols].astype(F32)
            total = acc[pl.ds(0, keep), cols] + got
            if last:
                grad[:, cols] = total
                new_master, _, _ = adam(total, master[:, cols], moment[:, cols], second[:, cols])
                hot_send[:, cols] = new_master.astype(BF16)
            else:
                sent = counts[s + 1] * unit
                acc[pl.ds(0, sent), cols] = total[:sent]
                rs_send[pl.ds(offset[s + 1], sent), cols] = total[sent:].astype(BF16)

        if last:
            for k in range(1, n_t):
                hot_copy(k, q).start()
            grad_store(q).start()
            hot_store(q).start()
        else:
            rs_copy(s + 1, q).start()

    cold_sent = 0
    for wave in range(CHUNKS + len(bits) - 1):
        for s in reversed(range(len(bits))):
            q = wave - s
            if 0 <= q < CHUNKS:
                settle(s, q)
        if cold_sent < CHUNKS:
            send_cold(cold_sent)
            cold_sent += 1

    for part in range(3):
        for copy in sel[part]:
            copy.wait_send()
    og_copy.wait_send()
    for q in range(CHUNKS):
        for s in range(len(bits)):
            rs_copy(s, q).wait_send()
        grad_store(q).wait()
        hot_store(q).wait()
        for k in range(1, n_t):
            hot_copy(k, q).wait()
        for slot in range(MOSTC):
            cold_copy(slot, True, q).wait()
            cold_copy(slot + COLD - MOSTC, False, q).wait()


def exchange(n_dp, n_t, outbox, cold_outbox, out_grad, master, moment, second):
    tok, qlocal = out_grad.shape
    unit = master.shape[0]
    units = n_dp // 2
    half = max(units // 2, 1)
    stages = max(n_dp.bit_length() - 2, 1)
    traded = (units - 1) * unit
    vmem = pl.BlockSpec(memory_space=pltpu.VMEM)
    anywhere = pl.BlockSpec(memory_space=pl.ANY)
    dma = pltpu.SemaphoreType.DMA
    return pl.pallas_call(
        functools.partial(exchange_kernel, n_dp, n_t),
        out_shape=(
            jax.ShapeDtypeStruct((unit, qlocal), F32),
            jax.ShapeDtypeStruct((unit, qlocal * n_t), BF16),
            jax.ShapeDtypeStruct((MOSTC, BLOCK, qlocal), BF16),
            jax.ShapeDtypeStruct((MOSTC, BLOCK, qlocal), BF16),
        ),
        in_specs=[vmem, vmem] + [anywhere] * 4,
        out_specs=[anywhere] * 4,
        scratch_shapes=[
            pltpu.VMEM((2, 2, tok, half * unit), BF16),
            pltpu.VMEM((tok, COLD * BLOCK), BF16),
            pltpu.VMEM((2 * tok, qlocal), BF16),
            pltpu.VMEM((2, half * unit, 2 * tok), BF16),
            pltpu.VMEM((COLD * BLOCK, tok), BF16),
            pltpu.VMEM((half * unit, qlocal), F32),
            pltpu.VMEM((traded, qlocal), BF16),
            pltpu.VMEM((traded, qlocal), BF16),
            pltpu.VMEM((COLD, BLOCK, qlocal), BF16),
            pltpu.VMEM((unit, qlocal), F32),
            pltpu.VMEM((unit, qlocal), F32),
            pltpu.VMEM((unit, qlocal), F32),
            pltpu.VMEM((unit, qlocal), F32),
            pltpu.VMEM((unit, qlocal), BF16),
            dma((4,)),
            dma((2, 3, n_t)),
            dma((2, 3, n_t)),
            dma(()),
            dma(()),
            dma((stages, CHUNKS)),
            dma((stages, CHUNKS)),
            dma((2, MOSTC, CHUNKS)),
            dma((2, MOSTC, CHUNKS)),
            dma((n_t, CHUNKS)),
            dma((n_t, CHUNKS)),
            dma((2, CHUNKS)),
        ],
        compiler_params=pltpu.CompilerParams(
            collective_id=0, has_side_effects=True, vmem_limit_bytes=60 * 1024 * 1024
        ),
    )(outbox, cold_outbox, out_grad, master, moment, second)


def cold_kernel(where_ref, owner_ref, prev_ref, next_ref, out_ref):
    c = pl.program_id(0)
    from_prev = owner_ref[where_ref[0], c] == 1
    from_next = owner_ref[where_ref[1], c] == 0
    total = jnp.where(from_prev, prev_ref[0].astype(F32), 0.0)
    out_ref[...] = total + jnp.where(from_next, next_ref[0].astype(F32), 0.0)


def ones_before(owner_ref, row, c):
    count = 0
    for b in range(COLD):
        count = count + jnp.where(b < c, owner_ref[row, b], 0)
    return count


def prev_slot(c, n, where_ref, owner_ref):
    return jnp.minimum(ones_before(owner_ref, where_ref[0], c), MOSTC - 1), 0, n


def next_slot(c, n, where_ref, owner_ref):
    row = where_ref[1]
    ones = ones_before(owner_ref, row, COLD)
    place = ones + c - ones_before(owner_ref, row, c)
    return jnp.clip(place - (COLD - MOSTC), 0, MOSTC - 1), 0, n


def merge_cold(where, owner_map, from_prev, from_next):
    qlocal = from_prev.shape[2]
    width = qlocal
    return pl.pallas_call(
        cold_kernel,
        out_shape=jax.ShapeDtypeStruct((COLD * BLOCK, qlocal), F32),
        grid_spec=pltpu.PrefetchScalarGridSpec(
            num_scalar_prefetch=2,
            grid=(COLD, 1),
            in_specs=[
                pl.BlockSpec((1, BLOCK, width), prev_slot),
                pl.BlockSpec((1, BLOCK, width), next_slot),
            ],
            out_specs=pl.BlockSpec((BLOCK, width), lambda c, n, *_: (c, n)),
        ),
    )(where, owner_map, from_prev, from_next)


def per_device(n_dp, n_t, activations, out_grad, block_ids, owner_map, master, moment, second):
    outbox, cold_outbox = gather(n_dp, n_t, master.shape[0], block_ids, owner_map, activations)
    grad, hot_weights, from_prev, from_next = exchange(
        n_dp, n_t, outbox, cold_outbox, out_grad, master, moment, second
    )
    index = lax.axis_index("dp")
    where = jnp.stack([(index + n_dp - 1) % n_dp, (index + 1) % n_dp]).astype(jnp.int32)
    cold_recv = merge_cold(where, owner_map, from_prev, from_next)
    new_master, new_moment, new_second = adam(grad, master, moment, second)
    return (new_master, new_moment, new_second, hot_weights, cold_recv)


def solution(mesh):
    return jax.shard_map(
        functools.partial(per_device, mesh.shape["dp"], mesh.shape["tensor"]),
        mesh=mesh,
        in_specs=(
            P(("dp", "tensor"), None),
            P("dp", "tensor"),
            P(),
            P(),
            P("dp", "tensor"),
            P("dp", "tensor"),
            P("dp", "tensor"),
        ),
        out_specs=(
            P("dp", "tensor"),
            P("dp", "tensor"),
            P("dp", "tensor"),
            P("dp", None),
            P("dp", "tensor"),
        ),
        check_vma=False,
    )
```

profile of v0, /device:TPU:1, one launch (start us, length us, event | category | flops | bytes accessed | tf_op | source)
XLA Modules:
  0.0 154.9 jit_solution(12534515412904382966)
XLA Ops:
  0.7 0.6 pad_add_fusion.where_ref
  1.2 1.3 copy.12.owner_ref
  2.6 3.3 %shard_map.110 = (bf16[2,2,4,96,256]{4,3,2,1,0:T(8,128)(2,1)}, bf16[4,96,512]{2,1,0:T(8,128)(2,1)}) custom-call(s32[4,12]{1,0:T(4,128)} %ids_ref.1, s32[8,4]{1,0:T(8,128)} %copy.12.owner_ref, bf16[96,16384]{1,0:T(8,128)(2,1)} %act.1), custom_call_target="tpu_custom_call" | custom-call | tf_op jit(solution)/shard_map/pallas_call | solution.py:105
  5.8 132.9 %shard_map.111 = (f32[128,4096]{1,0:T(8,128)}, bf16[128,16384]{1,0:T(8,128)(2,1)}, bf16[3,128,4096]{2,1,0:T(8,128)(2,1)}, bf16[3,128,4096]{2,1,0:T(8,128)(2,1)}) custom-call(bf16[2,2,4,96,256]{4,3,2,1,0:T(8,128)(2,1)} %get-tuple-element.11.outbox, bf16[4,96,512]{2,1,0:T(8,128)(2,1)} %get-tuple-element.12.cold_outbox, bf16[384,4096]{1,0:T(8,128)(2,1)} %og_hbm.1, ...), custom_call_target="tpu_custom_call" | custom-call | tf_op jit(solution)/shard_map/pallas_call | solution.py:406
  138.8 0.0 copy-start
  138.8 7.2 %shard_map.112 = f32[512,4096]{1,0:T(8,128)} custom-call(s32[2]{0:T(128)} %pad_add_fusion.where_ref, s32[8,4]{1,0:T(8,128)} %copy.12.owner_ref, bf16[3,128,4096]{2,1,0:T(8,128)(2,1)} %get-tuple-element.15.prev_ref, bf16[3,128,4096]{2,1,0:T(8,128)(2,1)} %get-tuple-element.16.next_ref), custom_call_target="tpu_custom_call" | custom-call | tf_op jit(solution)/shard_map/pallas_call | solution.py:479
  146.0 0.0 copy-done
  146.0 0.0 copy-start.1
  146.0 6.9 %multiply_subtract_fusion = (f32[128,4096]{1,0:T(8,128)}, f32[128,4096]{1,0:T(8,128)}, f32[128,4096]{1,0:T(8,128)}) fusion(f32[128,4096]{1,0:T(8,128)S(1)} %copy-done, f32[128,4096]{1,0:T(8,128)} %get-tuple-element.13, f32[128,4096]{1,0:T(8,128)} %moment_hbm.1, f32[128,4096]{1,0:T(8,128)} %second_hbm.1), kind=kLoop, calls=%fused_computation.2 | loop fusion | flops 7864320 | bytes 14680064 | tf_op jit(solution)/shard_map/sub | solution.py:33
  152.9 0.0 copy-done.1
  152.9 2.0 %copy.15 = bf16[128,16384]{1,0:T(8,128)(2,1)} copy(bf16[128,16384]{1,0:T(8,128)(2,1)S(1)} %copy-done.1) | data formatting | bytes 8388608
Async XLA Ops:
  138.8 7.2 %copy-start = (f32[128,4096]{1,0:T(8,128)S(1)}, f32[128,4096]{1,0:T(8,128)}, u32[]{:S(2)}) copy-start(f32[128,4096]{1,0:T(8,128)} %master_hbm.1) | copy-start | bytes 6291460
  146.0 6.9 %copy-start.1 = (bf16[128,16384]{1,0:T(8,128)(2,1)S(1)}, bf16[128,16384]{1,0:T(8,128)(2,1)}, u32[]{:S(2)}) copy-start(bf16[128,16384]{1,0:T(8,128)(2,1)} %get-tuple-element.28) | copy-start | bytes 12582916
where the time goes:
time: 157 us; the launch traced here: 155 us
  Pallas kernels  143 us (91%)
  other arithmetic  7.48 us (5%)
  local copies, waits for them, and re-layouts  3.37 us (2%)
    pallas_call x1, Pallas kernels, exchange(): pl.pallas_call(functools.partial(exchange_kernel, n_dp, n_t), out_shape=(...  133 us
    pallas_call x1, Pallas kernels, merge_cold(): pl.pallas_call(cold_kernel, out_shape=jax.ShapeDtypeStruct((COLD * BLOCK,...  7.21 us
    sub x1, other arithmetic, adam(): master - LEARN_RATE * (update + DECAY * master)  6.89 us
    unnamed x6, local copies, waits for them, and re-layouts  3.37 us
    pallas_call x1, Pallas kernels, gather(): pl.pallas_call(functools.partial(gather_kernel, n_dp, n_t, unit), out_sha...  3.25 us

commit v1 on v0

--- a/solution.py
+++ b/solution.py
@@ -317,15 +317,37 @@
     for load in loads[1:]:
         load.wait()
 
-    def hot_copy(k, q):
+    def hot_copy(up, d, q):
+        origin = t - (d - 1) if up else t + (d - 1)
+        cols = pl.ds(pl.multiple_of(origin * qlocal + q * chunk, chunk), chunk)
+        side = 0 if up else 1
         return pltpu.make_async_remote_copy(
-            src_ref=hot_send.at[:, pl.ds(q * chunk, chunk)],
-            dst_ref=hot_out.at[:, pl.ds(t * qlocal + q * chunk, chunk)],
-            send_sem=hot_send_sem.at[k, q],
-            recv_sem=hot_recv_sem.at[k, q],
-            device_id=(i, (t + k) % n_t),
+            src_ref=hot_send.at[:, pl.ds(q * chunk, chunk)] if d == 1 else hot_out.at[:, cols],
+            dst_ref=hot_out.at[:, cols],
+            send_sem=hot_send_sem.at[side, d, q],
+            recv_sem=hot_recv_sem.at[side, d, q],
+            device_id=(i, t + 1 if up else t - 1),
             device_id_type=MESH,
         )
+
+    def sends(up, d):
+        return (t >= d - 1) & (t < n_t - 1) if up else (t <= n_t - d) & (t > 0)
+
+    def gets(up, d):
+        return t >= d if up else t < n_t - d
+
+    def relay(d, q):
+        for up in (True, False):
+
+            @pl.when(gets(up, d))
+            def _():
+                hot_copy(up, d, q).wait_recv()
+
+            if d < n_t - 1:
+
+                @pl.when(sends(up, d + 1))
+                def _():
+                    hot_copy(up, d + 1, q).start()
 
     def grad_store(q):
         cols = pl.ds(q * chunk, chunk)
@@ -360,19 +382,27 @@
                 rs_send[pl.ds(offset[s + 1], sent), cols] = total[sent:].astype(BF16)
 
         if last:
-            for k in range(1, n_t):
-                hot_copy(k, q).start()
+            for up in (True, False):
+
+                @pl.when(sends(up, 1))
+                def _():
+                    hot_copy(up, 1, q).start()
+
             grad_store(q).start()
             hot_store(q).start()
         else:
             rs_copy(s + 1, q).start()
 
     cold_sent = 0
-    for wave in range(CHUNKS + len(bits) - 1):
+    ahead = len(bits) - 1
+    for wave in range(CHUNKS + ahead + n_t - 1):
         for s in reversed(range(len(bits))):
             q = wave - s
             if 0 <= q < CHUNKS:
                 settle(s, q)
+        for d in range(1, n_t):
+            if 0 <= wave - ahead - d < CHUNKS:
+                relay(d, wave - ahead - d)
         if cold_sent < CHUNKS:
             send_cold(cold_sent)
             cold_sent += 1
@@ -386,8 +416,13 @@
             rs_copy(s, q).wait_send()
         grad_store(q).wait()
         hot_store(q).wait()
-        for k in range(1, n_t):
-            hot_copy(k, q).wait()
+        for d in range(1, n_t):
+            for up in (True, False):
+
+                @pl.when(sends(up, d))
+                def _():
+                    hot_copy(up, d, q).wait_send()
+
         for slot in range(MOSTC):
             cold_copy(slot, True, q).wait()
             cold_copy(slot + COLD - MOSTC, False, q).wait()
@@ -437,8 +472,8 @@
             dma((stages, CHUNKS)),
             dma((2, MOSTC, CHUNKS)),
             dma((2, MOSTC, CHUNKS)),
-            dma((n_t, CHUNKS)),
-            dma((n_t, CHUNKS)),
+            dma((2, n_t, CHUNKS)),
+            dma((2, n_t, CHUNKS)),
             dma((2, CHUNKS)),
         ],
         compiler_params=pltpu.CompilerParams(

time: 157 us -> 164 us (1.045); the launches traced: 155 us -> 164 us
  Pallas kernels: 143 us -> 152 us
    pallas_call x1, Pallas kernels: 133 us -> 141 us  [exchange(): pl.pallas_call(functools.partial(exchange_kernel, n_dp, n_t), out_shape=(...]
where the time goes in v1:
time: 164 us
  Pallas kernels  152 us (93%)
  other arithmetic  7.48 us (5%)
  local copies, waits for them, and re-layouts  3.37 us (2%)
    pallas_call x1, Pallas kernels, exchange(): pl.pallas_call(functools.partial(exchange_kernel, n_dp, n_t), out_shape=(...  141 us
    pallas_call x1, Pallas kernels, merge_cold(): pl.pallas_call(cold_kernel, out_shape=jax.ShapeDtypeStruct((COLD * BLOCK,...  8.28 us
    sub x1, other arithmetic, adam(): master - LEARN_RATE * (update + DECAY * master)  6.89 us
    unnamed x6, local copies, waits for them, and re-layouts  3.37 us

profile of v1, /device:TPU:1, one launch (start us, length us, event | category | flops | bytes accessed | tf_op | source)
XLA Modules:
  0.0 163.8 jit_solution(13602831529786234294)
XLA Ops:
  0.7 0.6 pad_add_fusion.where_ref
  1.2 1.3 copy.12.owner_ref
  2.6 3.3 %shard_map.110 = (bf16[2,2,4,96,256]{4,3,2,1,0:T(8,128)(2,1)}, bf16[4,96,512]{2,1,0:T(8,128)(2,1)}) custom-call(s32[4,12]{1,0:T(4,128)} %ids_ref.1, s32[8,4]{1,0:T(8,128)} %copy.12.owner_ref, bf16[96,16384]{1,0:T(8,128)(2,1)} %act.1), custom_call_target="tpu_custom_call" | custom-call | tf_op jit(solution)/shard_map/pallas_call | solution.py:105
  5.8 140.7 %shard_map.111 = (f32[128,4096]{1,0:T(8,128)}, bf16[128,16384]{1,0:T(8,128)(2,1)}, bf16[3,128,4096]{2,1,0:T(8,128)(2,1)}, bf16[3,128,4096]{2,1,0:T(8,128)(2,1)}) custom-call(bf16[2,2,4,96,256]{4,3,2,1,0:T(8,128)(2,1)} %get-tuple-element.11.outbox, bf16[4,96,512]{2,1,0:T(8,128)(2,1)} %get-tuple-element.12.cold_outbox, bf16[384,4096]{1,0:T(8,128)(2,1)} %og_hbm.1, ...), custom_call_target="tpu_custom_call" | custom-call | tf_op jit(solution)/shard_map/pallas_call | solution.py:441
  146.6 0.0 copy-start
  146.6 8.3 %shard_map.112 = f32[512,4096]{1,0:T(8,128)} custom-call(s32[2]{0:T(128)} %pad_add_fusion.where_ref, s32[8,4]{1,0:T(8,128)} %copy.12.owner_ref, bf16[3,128,4096]{2,1,0:T(8,128)(2,1)} %get-tuple-element.15.prev_ref, bf16[3,128,4096]{2,1,0:T(8,128)(2,1)} %get-tuple-element.16.next_ref), custom_call_target="tpu_custom_call" | custom-call | tf_op jit(solution)/shard_map/pallas_call | solution.py:514
  154.9 0.0 copy-done
  154.9 0.0 copy-start.1
  154.9 6.9 %multiply_subtract_fusion = (f32[128,4096]{1,0:T(8,128)}, f32[128,4096]{1,0:T(8,128)}, f32[128,4096]{1,0:T(8,128)}) fusion(f32[128,4096]{1,0:T(8,128)S(1)} %copy-done, f32[128,4096]{1,0:T(8,128)} %get-tuple-element.13, f32[128,4096]{1,0:T(8,128)} %moment_hbm.1, f32[128,4096]{1,0:T(8,128)} %second_hbm.1), kind=kLoop, calls=%fused_computation.2 | loop fusion | flops 7864320 | bytes 14680064 | tf_op jit(solution)/shard_map/sub | solution.py:33
  161.8 0.0 copy-done.1
  161.8 2.0 %copy.15 = bf16[128,16384]{1,0:T(8,128)(2,1)} copy(bf16[128,16384]{1,0:T(8,128)(2,1)S(1)} %copy-done.1) | data formatting | bytes 8388608
Async XLA Ops:
  146.6 8.3 %copy-start = (f32[128,4096]{1,0:T(8,128)S(1)}, f32[128,4096]{1,0:T(8,128)}, u32[]{:S(2)}) copy-start(f32[128,4096]{1,0:T(8,128)} %master_hbm.1) | copy-start | bytes 6291460
  154.9 6.9 %copy-start.1 = (bf16[128,16384]{1,0:T(8,128)(2,1)S(1)}, bf16[128,16384]{1,0:T(8,128)(2,1)}, u32[]{:S(2)}) copy-start(bf16[128,16384]{1,0:T(8,128)(2,1)} %get-tuple-element.28) | copy-start | bytes 12582916

commit v2 on v0

v2 whole, which is shorter than its diff:
```python
import functools

import jax
import jax.numpy as jnp
from jax import lax
from jax.experimental import pallas as pl
from jax.experimental.pallas import tpu as pltpu
from jax.sharding import PartitionSpec as P

BLOCK = 128
HOT = 8
COLD = 4
MOSTC = 3

BETA_ONE = 0.9
BETA_TWO = 0.95
ADAM_EPS = 1e-08
LEARN_RATE = 0.01
DECAY = 0.1
CORRECT_ONE = 1.0 - 0.9**10
CORRECT_TWO = 1.0 - 0.95**10

CHUNKS = 16
EARLY = 5
COLD_AT = 1
COLD_LAG = 3
MESH = pl.DeviceIdType.MESH
F32 = jnp.float32
BF16 = jnp.bfloat16


def adam(grad, master, moment, second):
    new_moment = BETA_ONE * moment + (1.0 - BETA_ONE) * grad
    new_second = BETA_TWO * second + (1.0 - BETA_TWO) * grad * grad
    update = new_moment / CORRECT_ONE / (jnp.sqrt(new_second / CORRECT_TWO) + ADAM_EPS)
    return master - LEARN_RATE * (update + DECAY * master), new_moment, new_second


def stage_bits(n_dp):
    bits = [1]
    bit = 4
    while bit < n_dp:
        bits.append(bit)
        bit *= 2
    return bits


def flip(d, bit):
    return d + bit - 2 * bit * ((d // bit) % 2)


def side_block(n_dp, unit, side, col):
    place = col // unit
    d = (place // 2) * 4 + side * 2 + place % 2
    return (d * unit + col % unit) // BLOCK


def gather_kernel(n_dp, n_t, unit, ids_ref, owner_ref, act, outbox, cold_outbox, sem):
    i = lax.axis_index("dp")
    t = lax.axis_index("tensor")
    side = (i // 2) % 2
    wide = outbox.shape[3] // BLOCK
    owned = [owner_ref[c, i] for c in range(COLD)]
    ones = owned[0]
    for c in range(1, COLD):
        ones = ones + owned[c]
    place, taken, left = [], 0, ones
    for c in range(COLD):
        place.append(jnp.where(owned[c] == 1, taken, left))
        taken, left = taken + owned[c], left + 1 - owned[c]

    copies = []

    def pull(block, target):
        cols = pl.ds(pl.multiple_of(block * BLOCK, BLOCK), BLOCK)
        copies.append(pltpu.make_async_copy(act.at[:, cols], target, sem.at[len(copies)]))
        copies[-1].start()

    for which in (1, 0):
        for k in range(n_t):
            group = (t + k) % n_t
            for b in range(wide):
                index = side_block(n_dp, unit, (side + which) % 2, b * BLOCK)
                pull(ids_ref[group, index], outbox.at[which, k, :, pl.ds(b * BLOCK, BLOCK)])
    for k in range(n_t):
        group = (t + k) % n_t
        for p in range(COLD):
            block = 0
            for c in range(COLD):
                block = block + jnp.where(place[c] == p, ids_ref[group, HOT + c], 0)
            pull(block, cold_outbox.at[k, :, pl.ds(p * BLOCK, BLOCK)])
    for copy in copies:
        copy.wait()


def gather(n_dp, n_t, unit, ids, owner_t, activations):
    rows_tok = activations.shape[0]
    wide = n_dp // 2 * unit
    smem = pl.BlockSpec(memory_space=pltpu.SMEM)
    vmem = pl.BlockSpec(memory_space=pltpu.VMEM)
    jobs = n_t * (2 * wide // BLOCK + COLD)
    return pl.pallas_call(
        functools.partial(gather_kernel, n_dp, n_t, unit),
        out_shape=(
            pltpu.VMEM((2, n_t, rows_tok, wide), BF16),
            pltpu.VMEM((n_t, rows_tok, COLD * BLOCK), BF16),
        ),
        in_specs=[smem, smem, pl.BlockSpec(memory_space=pltpu.HBM)],
        out_specs=[vmem, vmem],
        scratch_shapes=[pltpu.SemaphoreType.DMA((jobs,))],
        compiler_params=pltpu.CompilerParams(vmem_limit_bytes=61 * 1024 * 1024),
    )(ids, owner_t, activations)


def exchange_kernel(
    n_dp,
    n_t,
    owner_ref,
    outbox,
    cold_outbox,
    og_hbm,
    master_hbm,
    moment_hbm,
    second_hbm,
    master,
    moment,
    second,
    hot,
    cold,
    inbox,
    cold_inbox,
    part_inbox,
    part_cold,
    peer_cold,
    og,
    flat,
    lhs,
    cold_lhs,
    acc,
    rs_send,
    rs_recv,
    og_load_sem,
    load_sem,
    sel_send_sem,
    sel_recv_sem,
    pass_send_sem,
    pass_recv_sem,
    cold_send_sem,
    cold_recv_sem,
    peer_send_sem,
    peer_recv_sem,
    og_send_sem,
    og_recv_sem,
    rs_send_sem,
    rs_recv_sem,
    hot_send_sem,
    hot_recv_sem,
):
    i = lax.axis_index("dp")
    t = lax.axis_index("tensor")
    odd = i % 2
    peer = flip(i, 1)
    nxt, prv = (i + 1) % n_dp, (i + n_dp - 1) % n_dp
    part = (i + n_dp + 2 * odd - 1) % n_dp
    bits = stage_bits(n_dp)
    stages = len(bits)
    side_units = n_dp // 2
    unit = master.shape[1]
    wide = side_units * unit
    rows_tok = cold_outbox.shape[1]
    tok = og.shape[1] // 3
    chunk = og.shape[2]

    def cut(ref, q):
        return ref.at[:, pl.ds(pl.multiple_of(q * chunk, chunk), chunk)]

    def og_load(q):
        return pltpu.make_async_copy(
            cut(og_hbm, q), og.at[q, pl.ds(0, tok)], og_load_sem.at[q]
        )

    @pl.loop(0, CHUNKS)
    def _(q):
        og_load(q).start()

    def state_load(which, q):
        source = (master_hbm, moment_hbm, second_hbm)[which]
        target = (master, moment, second)[which]
        return pltpu.make_async_copy(cut(source, q), target.at[q], load_sem.at[which, q])

    partners = [(flip(i, b), t) for b in bits] + [(part, t)]
    partners += [(i, (t + k) % n_t) for k in range(1, n_t)]
    barrier = pltpu.get_barrier_semaphore()
    for partner in partners:
        pl.semaphore_signal(barrier, inc=1, device_id=partner, device_id_type=MESH)

    mine = pl.ds(t * rows_tok, rows_tok)

    def sel_copy(which, k):
        return pltpu.make_async_remote_copy(
            src_ref=outbox.at[which, k],
            dst_ref=inbox.at[which, mine],
            send_sem=sel_send_sem.at[which, k],
            recv_sem=sel_recv_sem.at[which, k],
            device_id=(i, (t + k) % n_t),
            device_id_type=MESH,
        )

    def cold_sel_copy(k):
        return pltpu.make_async_remote_copy(
            src_ref=cold_outbox.at[k],
            dst_ref=cold_inbox.at[mine],
            send_sem=sel_send_sem.at[2, k],
            recv_sem=sel_recv_sem.at[2, k],
            device_id=(i, (t + k) % n_t),
            device_id_type=MESH,
        )

    def pass_copy(k):
        rows = pl.ds(((t + n_t - k) % n_t) * rows_tok, rows_tok)
        return pltpu.make_async_remote_copy(
            src_ref=inbox.at[1, rows],
            dst_ref=part_inbox.at[rows],
            send_sem=pass_send_sem.at[k],
            recv_sem=pass_recv_sem.at[k],
            device_id=(part, t),
            device_id_type=MESH,
        )

    def og_copy(q):
        return pltpu.make_async_remote_copy(
            src_ref=og.at[q, pl.ds(0, tok)],
            dst_ref=og.at[q, pl.ds(tok, tok)],
            send_sem=og_send_sem.at[q],
            recv_sem=og_recv_sem.at[q],
            device_id=(part, t),
            device_id_type=MESH,
        )

    og_peer_copy = pltpu.make_async_remote_copy(
        src_ref=og.at[:, pl.ds(0, tok)],
        dst_ref=og.at[:, pl.ds(2 * tok, tok)],
        send_sem=peer_send_sem.at[0],
        recv_sem=peer_recv_sem.at[0],
        device_id=(peer, t),
        device_id_type=MESH,
    )

    inbox[1, mine] = outbox[1, 0]
    inbox[0, mine] = outbox[0, 0]
    cold_inbox[mine] = cold_outbox[0]
    pl.semaphore_wait(barrier, len(partners))
    for k in range(1, n_t):
        sel_copy(1, k).start()
    og_load(0).wait()
    og_copy(0).start()
    pass_copy(0).start()
    for k in range(1, n_t):
        sel_copy(0, k).start()
    for k in range(1, n_t):
        cold_sel_copy(k).start()

    @pl.loop(1, CHUNKS)
    def _(q):
        og_load(q).wait()

    og_peer_copy.start()

    @pl.loop(0, CHUNKS)
    def _(q):
        for which in range(3):
            state_load(which, q).start()

    for k in range(1, n_t):
        sel_copy(1, k).wait_recv()
        pass_copy(k).start()
        og_copy(k).start()
    for q in range(n_t, EARLY):
        og_copy(q).start()
    for k in range(1, n_t):
        sel_copy(0, k).wait_recv()

    def unit_at(r):
        d = i
        for index, b in enumerate(bits):
            if r & (1 << (stages - 1 - index)):
                d = flip(d, b)
        return d

    def build_hot(first, source):
        depth = pl.ds(first, tok)
        flat[:, depth] = source[...].T
        for r in range(side_units):
            d = unit_at(r)
            rows = pl.ds(pl.multiple_of(((d // 4) * 2 + d % 2) * unit, unit), unit)
            lhs[pl.ds(r * unit, unit), depth] = flat[rows, depth]

    build_hot(0, inbox.at[0])
    for k in range(n_t):
        pass_copy(k).wait_recv()
    build_hot(tok, part_inbox)

    counts = [side_units >> (s + 1) for s in range(stages)]
    offset = [sum(counts[:s]) * unit for s in range(stages)]
    early = max(EARLY, n_t)

    def rs_copy(s, q):
        place_ = (q, pl.ds(offset[s], counts[s] * unit))
        return pltpu.make_async_remote_copy(
            src_ref=rs_send.at[place_],
            dst_ref=rs_recv.at[place_],
            send_sem=rs_send_sem.at[s, q],
            recv_sem=rs_recv_sem.at[s, q],
            device_id=(flip(i, bits[s]), t),
            device_id_type=MESH,
        )

    def hot_copy(up, d, q):
        origin = t - (d - 1) if up else t + (d - 1)
        side = 0 if up else 1
        return pltpu.make_async_remote_copy(
            src_ref=hot.at[origin, q],
            dst_ref=hot.at[origin, q],
            send_sem=hot_send_sem.at[side, d, q],
            recv_sem=hot_recv_sem.at[side, d, q],
            device_id=(i, t + 1 if up else t - 1),
            device_id_type=MESH,
        )

    def sends(up, d):
        return (t >= d - 1) & (t < n_t - 1) if up else (t <= n_t - d) & (t > 0)

    def cold_pass_copy(to_part):
        first = (1 - odd) if to_part else odd
        which = 0 if to_part else 1
        return pltpu.make_async_remote_copy(
            src_ref=cold_inbox.at[:, pl.ds(pl.multiple_of(first * BLOCK, BLOCK), MOSTC * BLOCK)],
            dst_ref=part_cold if to_part else peer_cold,
            send_sem=cold_send_sem.at[which],
            recv_sem=cold_recv_sem.at[which],
            device_id=(part if to_part else peer, t),
            device_id_type=MESH,
        )

    def ones_before(row, c):
        count = 0
        for b in range(c):
            count = count + owner_ref[b, row]
        return count

    def build_cold():
        for place_, source, row, is_prev in (
            (0, part_cold, part, 1 - odd),
            (1, peer_cold, peer, odd),
        ):
            slots = [source[:, pl.ds(p * BLOCK, BLOCK)].astype(F32) for p in range(MOSTC)]
            for c in range(COLD):
                before = ones_before(row, c)
                after = ones_before(row, COLD) + c - before - (COLD - MOSTC)
                slot = before * is_prev + after * (1 - is_prev)
                taken = jnp.where(owner_ref[c, row] == is_prev, 1.0, 0.0)
                cols = jnp.zeros((tok, BLOCK), F32)
                for p in range(MOSTC):
                    cols = cols + slots[p] * (jnp.where(slot == p, 1.0, 0.0) * taken)
                cold_lhs[pl.ds(c * BLOCK, BLOCK), pl.ds(place_ * tok, tok)] = cols.astype(BF16).T

    keep = counts[0] * unit

    def products(q):
        og_copy(q).wait_recv()
        out = jnp.dot(lhs[...], og[q, pl.ds(0, 2 * tok)], preferred_element_type=F32)
        rs_send[q, pl.ds(0, keep)] = out[keep:].astype(BF16)
        rs_copy(0, q).start()
        acc[q] = out[:keep]

    def cold_products(q):
        cold[q] = jnp.dot(cold_lhs[...], og[q, pl.ds(tok, 2 * tok)], preferred_element_type=F32)

    def settle(s, q):
        rs_copy(s, q).wait_recv()
        held = counts[s] * unit
        got = rs_recv[q, pl.ds(offset[s], held)].astype(F32)
        total = acc[q, pl.ds(0, held)] + got
        if s < stages - 1:
            sent = counts[s + 1] * unit
            rs_send[q, pl.ds(offset[s + 1], sent)] = total[sent:].astype(BF16)
            rs_copy(s + 1, q).start()
            acc[q, pl.ds(0, sent)] = total[:sent]
            return
        for which in range(3):
            state_load(which, q).wait()
        new_master, new_moment, new_second = adam(total, master[q], moment[q], second[q])
        hot[t, q] = new_master.astype(BF16)
        for up in (True, False):

            @pl.when(sends(up, 1))
            def _():
                hot_copy(up, 1, q).start()

        master[q] = new_master
        moment[q] = new_moment
        second[q] = new_second

    def relay(up, d, q):
        @pl.when(sends(up, d + 1))
        def _():
            hot_copy(up, d, q).wait_recv()
            hot_copy(up, d + 1, q).start()

    def inside(q):
        return (q >= 0) & (q < CHUNKS)

    ticks = CHUNKS + max(stages + n_t - 2, COLD_LAG)

    @pl.loop(0, ticks)
    def _(tick):
        for s in reversed(range(stages)):
            q = tick - 1 - s

            @pl.when(inside(q))
            def _():
                settle(s, q)

        for d in range(1, n_t - 1):
            q = tick - stages - d

            @pl.when(inside(q))
            def _():
                relay(True, d, q)
                relay(False, d, q)

        @pl.when(tick == COLD_AT)
        def _():
            for k in range(1, n_t):
                cold_sel_copy(k).wait_recv()
            cold_pass_copy(True).start()
            cold_pass_copy(False).start()

        @pl.when(tick == COLD_LAG)
        def _():
            og_peer_copy.wait_recv()
            cold_pass_copy(True).wait_recv()
            cold_pass_copy(False).wait_recv()
            build_cold()

        @pl.when(tick + early < CHUNKS)
        def _():
            og_copy(tick + early).start()

        @pl.when(tick < CHUNKS)
        def _():
            products(tick)

        q = tick - COLD_LAG

        @pl.when(inside(q))
        def _():
            cold_products(q)

    for k in range(1, n_t):
        sel_copy(0, k).wait_send()
        sel_copy(1, k).wait_send()
        cold_sel_copy(k).wait_send()
    for k in range(n_t):
        pass_copy(k).wait_send()
    og_peer_copy.wait_send()
    cold_pass_copy(True).wait_send()
    cold_pass_copy(False).wait_send()

    @pl.loop(0, CHUNKS)
    def _(q):
        og_copy(q).wait_send()
        for s in range(stages):
            rs_copy(s, q).wait_send()
        for d in range(1, n_t):
            for up in (True, False):

                @pl.when(sends(up, d))
                def _():
                    hot_copy(up, d, q).wait_send()

                @pl.when(t == n_t - 1 if up else t == 0)
                def _():
                    hot_copy(up, d, q).wait_recv()


def exchange(n_dp, n_t, owner_t, outbox, cold_outbox, out_grad, master, moment, second):
    rows_tok = cold_outbox.shape[1]
    tok, qlocal = out_grad.shape
    unit = master.shape[0]
    chunk = qlocal // CHUNKS
    side_units = n_dp // 2
    wide = side_units * unit
    stages = len(stage_bits(n_dp))
    traded = (side_units - 1) * unit
    smem = pl.BlockSpec(memory_space=pltpu.SMEM)
    vmem = pl.BlockSpec(memory_space=pltpu.VMEM)
    hbm = pl.BlockSpec(memory_space=pltpu.HBM)
    dma = pltpu.SemaphoreType.DMA
    return pl.pallas_call(
        functools.partial(exchange_kernel, n_dp, n_t),
        out_shape=(
            pltpu.VMEM((CHUNKS, unit, chunk), F32),
            pltpu.VMEM((CHUNKS, unit, chunk), F32),
            pltpu.VMEM((CHUNKS, unit, chunk), F32),
            pltpu.VMEM((n_t, CHUNKS, unit, chunk), BF16),
            pltpu.VMEM((CHUNKS, COLD * BLOCK, chunk), F32),
        ),
        in_specs=[smem, vmem, vmem] + [hbm] * 4,
        out_specs=[vmem] * 5,
        scratch_shapes=[
            pltpu.VMEM((2, tok, wide), BF16),
            pltpu.VMEM((tok, COLD * BLOCK), BF16),
            pltpu.VMEM((tok, wide), BF16),
            pltpu.VMEM((tok, MOSTC * BLOCK), BF16),
            pltpu.VMEM((tok, MOSTC * BLOCK), BF16),
            pltpu.VMEM((CHUNKS, 3 * tok, chunk), BF16),
            pltpu.VMEM((wide, 2 * tok), BF16),
            pltpu.VMEM((wide, 2 * tok), BF16),
            pltpu.VMEM((COLD * BLOCK, 2 * tok), BF16),
            pltpu.VMEM((CHUNKS, wide // 2, chunk), F32),
            pltpu.VMEM((CHUNKS, traded, chunk), BF16),
            pltpu.VMEM((CHUNKS, traded, chunk), BF16),
            dma((CHUNKS,)),
            dma((3, CHUNKS)),
            dma((3, n_t)),
            dma((3, n_t)),
            dma((n_t,)),
            dma((n_t,)),
            dma((2,)),
            dma((2,)),
            dma((1,)),
            dma((1,)),
            dma((CHUNKS,)),
            dma((CHUNKS,)),
            dma((stages, CHUNKS)),
            dma((stages, CHUNKS)),
            dma((2, n_t, CHUNKS)),
            dma((2, n_t, CHUNKS)),
        ],
        compiler_params=pltpu.CompilerParams(
            collective_id=0, has_side_effects=True, vmem_limit_bytes=42 * 1024 * 1024
        ),
    )(owner_t, outbox, cold_outbox, out_grad, master, moment, second)


def place_kernel(n_t, master, moment, second, hot, cold, *refs):
    outs, sem = refs[:5], refs[5]
    chunk = master.shape[2]

    jobs = [(4, 0)] + [(w, 0) for w in range(3)] + [(3, g) for g in range(n_t)]

    def all_of(act):
        @pl.loop(0, CHUNKS)
        def _(q):
            for which, g in jobs:
                slot = which if which < 3 else (3 if which == 4 else 4 + g)
                source = (master, moment, second, hot.at[g], cold)[which]
                cols = pl.ds(pl.multiple_of((g * CHUNKS + q) * chunk, chunk), chunk)
                act(
                    pltpu.make_async_copy(
                        source.at[q], outs[which].at[:, cols], sem.at[slot, q]
                    )
                )

    all_of(lambda copy: copy.start())
    all_of(lambda copy: copy.wait())


def place_out(n_t, parts):
    chunks, unit, chunk = parts[0].shape
    qlocal = chunks * chunk
    vmem = pl.BlockSpec(memory_space=pltpu.VMEM)
    hbm = pl.BlockSpec(memory_space=pltpu.HBM)
    return pl.pallas_call(
        functools.partial(place_kernel, n_t),
        out_shape=(
            jax.ShapeDtypeStruct((unit, qlocal), F32),
            jax.ShapeDtypeStruct((unit, qlocal), F32),
            jax.ShapeDtypeStruct((unit, qlocal), F32),
            jax.ShapeDtypeStruct((unit, qlocal * n_t), BF16),
            jax.ShapeDtypeStruct((parts[4].shape[1], qlocal), F32),
        ),
        in_specs=[vmem] * 5,
        out_specs=[hbm] * 5,
        scratch_shapes=[pltpu.SemaphoreType.DMA((4 + n_t, CHUNKS))],
        compiler_params=pltpu.CompilerParams(vmem_limit_bytes=40 * 1024 * 1024),
    )(*parts)


def per_device(n_dp, n_t, activations, out_grad, block_ids, owner_map, master, moment, second):
    owner_t = owner_map.T
    outbox, cold_outbox = gather(n_dp, n_t, master.shape[0], block_ids, owner_t, activations)
    parts = exchange(
        n_dp, n_t, owner_t, outbox, cold_outbox, out_grad, master, moment, second
    )
    return tuple(place_out(n_t, parts))


def solution(mesh):
    return jax.shard_map(
        functools.partial(per_device, mesh.shape["dp"], mesh.shape["tensor"]),
        mesh=mesh,
        in_specs=(
            P(("dp", "tensor"), None),
            P("dp", "tensor"),
            P(),
            P(),
            P("dp", "tensor"),
            P("dp", "tensor"),
            P("dp", "tensor"),
        ),
        out_specs=(
            P("dp", "tensor"),
            P("dp", "tensor"),
            P("dp", "tensor"),
            P("dp", None),
            P("dp", "tensor"),
        ),
        check_vma=False,
    )
```

time: 157 us -> 140 us (0.89)
  Pallas kernels: 143 us -> 134 us
  other arithmetic: 7.48 us -> 0 us
    pallas_call x1, Pallas kernels: 133 us -> 120 us  [exchange(): pl.pallas_call(functools.partial(exchange_kernel, n_dp, n_t), out_shape=(...]
    sub x1 -> x0, other arithmetic: 6.89 us -> none  [adam(): master - LEARN_RATE * (update + DECAY * master)]
    pallas_call x1, Pallas kernels: 7.21 us -> 10.9 us  [place_out(): pl.pallas_call(functools.partial(place_kernel, n_t), out_shape=(jax.Shape...]
where the time goes in v2:
time: 140 us; the launch traced here: 139 us
  Pallas kernels  134 us (96%)
  local copies, waits for them, and re-layouts  4.83 us (3%)
    pallas_call x1, Pallas kernels, exchange(): pl.pallas_call(functools.partial(exchange_kernel, n_dp, n_t), out_shape=(...  120 us
    pallas_call x1, Pallas kernels, place_out(): pl.pallas_call(functools.partial(place_kernel, n_t), out_shape=(jax.Shape...  10.9 us
    unnamed x6, local copies, waits for them, and re-layouts  4.83 us

profile of v2, /device:TPU:1, one launch (start us, length us, event | category | flops | bytes accessed | tf_op | source)
XLA Modules:
  0.0 139.3 jit_solution(10807038332330688658)
XLA Ops:
  0.6 2.5 %shard_map.110 = (bf16[2,4,96,512]{3,2,1,0:T(8,128)(2,1)S(1)}, bf16[4,96,512]{2,1,0:T(8,128)(2,1)S(1)}) custom-call(s32[4,12]{1,0:T(4,128)} %ids_ref.1, s32[4,8]{1,0:T(4,128)} %bitcast.1, bf16[96,16384]{1,0:T(8,128)(2,1)} %act.1), custom_call_target="tpu_custom_call" | custom-call | tf_op jit(solution)/shard_map/pallas_call | solution.py:102
  3.1 0.0 copy-start.1
  3.1 0.9 copy-done.1
  4.0 0.0 copy-start.2
  4.0 0.7 copy-done.2
  4.7 120.5 %shard_map.111 = (f32[16,128,256]{2,1,0:T(8,128)S(1)}, f32[16,128,256]{2,1,0:T(8,128)S(1)}, f32[16,128,256]{2,1,0:T(8,128)S(1)}, bf16[4,16,128,256]{3,2,1,0:T(8,128)(2,1)S(1)}, f32[16,512,256]{2,1,0:T(8,128)S(1)}) custom-call(s32[4,8]{1,0:T(4,128)} %bitcast.2, bf16[2,4,96,512]{3,2,1,0:T(8,128)(2,1)} %copy-done.1, bf16[4,96,512]{2,1,0:T(8,128)(2,1)} %copy-done.2, ...), custom_call_target="tpu_custom_call" | custom-call | tf_op jit(solution)/shard_map/pallas_call | solution.py:500
  125.2 0.0 copy-start
  125.3 3.2 %copy-done = f32[16,512,256]{2,1,0:T(8,128)} copy-done((f32[16,512,256]{2,1,0:T(8,128)}, f32[16,512,256]{2,1,0:T(8,128)S(1)}, u32[]{:S(2)}) %copy-start) | copy-done | bytes 8388632
  128.5 10.9 %shard_map.112 = (f32[128,4096]{1,0:T(8,128)}, f32[128,4096]{1,0:T(8,128)}, f32[128,4096]{1,0:T(8,128)}, bf16[128,16384]{1,0:T(8,128)(2,1)}, f32[512,4096]{1,0:T(8,128)}) custom-call(f32[16,128,256]{2,1,0:T(8,128)S(1)} %get-tuple-element.14.master, f32[16,128,256]{2,1,0:T(8,128)S(1)} %get-tuple-element.15.moment, ...), custom_call_target="tpu_custom_call" | custom-call | tf_op jit(solution)/shard_map/pallas_call | solution.py:575
Async XLA Ops:
  3.1 0.9 copy-start.1
  4.0 0.7 copy-start.2
  125.2 3.2 %copy-start = (f32[16,512,256]{2,1,0:T(8,128)}, f32[16,512,256]{2,1,0:T(8,128)S(1)}, u32[]{:S(2)}) copy-start(f32[16,512,256]{2,1,0:T(8,128)S(1)} %get-tuple-element.18.cold) | copy-start | bytes 25165828

commit v3 on v2

--- a/solution.py
+++ b/solution.py
@@ -21,9 +21,12 @@
 CORRECT_TWO = 1.0 - 0.95**10
 
 CHUNKS = 16
-EARLY = 5
-COLD_AT = 1
-COLD_LAG = 3
+EARLY = 4
+SETTLE_LAG = 1
+RELAY_LAG = 1
+REACH = 2
+COLD_AT = 3
+COLD_LAG = CHUNKS // 2
 MESH = pl.DeviceIdType.MESH
 F32 = jnp.float32
 BF16 = jnp.bfloat16
@@ -250,14 +253,16 @@
     inbox[0, mine] = outbox[0, 0]
     cold_inbox[mine] = cold_outbox[0]
     pl.semaphore_wait(barrier, len(partners))
-    for k in range(1, n_t):
+    lower = t < n_t // 2
+    far = [jnp.where(lower, k, n_t - k) for k in range(n_t - 1, 0, -1)]
+    for k in far:
         sel_copy(1, k).start()
     og_load(0).wait()
     og_copy(0).start()
     pass_copy(0).start()
-    for k in range(1, n_t):
+    for k in far:
         sel_copy(0, k).start()
-    for k in range(1, n_t):
+    for k in far:
         cold_sel_copy(k).start()
 
     @pl.loop(1, CHUNKS)
@@ -271,11 +276,12 @@
         for which in range(3):
             state_load(which, q).start()
 
-    for k in range(1, n_t):
+    og_copy(0).wait_recv()
+    og_copy(1).start()
+    for k in far:
         sel_copy(1, k).wait_recv()
         pass_copy(k).start()
-        og_copy(k).start()
-    for q in range(n_t, EARLY):
+    for q in range(2, EARLY):
         og_copy(q).start()
     for k in range(1, n_t):
         sel_copy(0, k).wait_recv()
@@ -302,7 +308,6 @@
 
     counts = [side_units >> (s + 1) for s in range(stages)]
     offset = [sum(counts[:s]) * unit for s in range(stages)]
-    early = max(EARLY, n_t)
 
     def rs_copy(s, q):
         place_ = (q, pl.ds(offset[s], counts[s] * unit))
@@ -316,19 +321,30 @@
         )
 
     def hot_copy(up, d, q):
-        origin = t - (d - 1) if up else t + (d - 1)
+        step = d if d <= REACH else 1
+        origin = t if d <= REACH else (t - (d - 1) if up else t + (d - 1))
         side = 0 if up else 1
         return pltpu.make_async_remote_copy(
             src_ref=hot.at[origin, q],
             dst_ref=hot.at[origin, q],
             send_sem=hot_send_sem.at[side, d, q],
             recv_sem=hot_recv_sem.at[side, d, q],
-            device_id=(i, t + 1 if up else t - 1),
+            device_id=(i, t + step if up else t - step),
             device_id_type=MESH,
         )
 
+    def gets(up, d):
+        return t >= d if up else t < n_t - d
+
     def sends(up, d):
+        if d <= REACH:
+            return t < n_t - d if up else t >= d
         return (t >= d - 1) & (t < n_t - 1) if up else (t <= n_t - d) & (t > 0)
+
+    def waits_late(up, d):
+        if d < REACH:
+            return gets(up, d)
+        return gets(up, d) & (t == n_t - 1 if up else t == 0)
 
     def cold_pass_copy(to_part):
         first = (1 - odd) if to_part else odd
@@ -367,7 +383,11 @@
     keep = counts[0] * unit
 
     def products(q):
-        og_copy(q).wait_recv()
+
+        @pl.when(q > 0)
+        def _():
+            og_copy(q).wait_recv()
+
         out = jnp.dot(lhs[...], og[q, pl.ds(0, 2 * tok)], preferred_element_type=F32)
         rs_send[q, pl.ds(0, keep)] = out[keep:].astype(BF16)
         rs_copy(0, q).start()
@@ -391,11 +411,12 @@
             state_load(which, q).wait()
         new_master, new_moment, new_second = adam(total, master[q], moment[q], second[q])
         hot[t, q] = new_master.astype(BF16)
-        for up in (True, False):
-
-            @pl.when(sends(up, 1))
-            def _():
-                hot_copy(up, 1, q).start()
+        for d in range(1, min(REACH + 1, n_t)):
+            for up in (True, False):
+
+                @pl.when(sends(up, d))
+                def _():
+                    hot_copy(up, d, q).start()
 
         master[q] = new_master
         moment[q] = new_moment
@@ -410,19 +431,20 @@
     def inside(q):
         return (q >= 0) & (q < CHUNKS)
 
-    ticks = CHUNKS + max(stages + n_t - 2, COLD_LAG)
+    settled = 1 + (stages - 1) * SETTLE_LAG
+    ticks = CHUNKS + settled + max(n_t - 1 - REACH, 0) * RELAY_LAG
 
     @pl.loop(0, ticks)
     def _(tick):
         for s in reversed(range(stages)):
-            q = tick - 1 - s
+            q = tick - 1 - s * SETTLE_LAG
 
             @pl.when(inside(q))
             def _():
                 settle(s, q)
 
-        for d in range(1, n_t - 1):
-            q = tick - stages - d
+        for d in range(REACH, n_t - 1):
+            q = tick - settled - (d - REACH + 1) * RELAY_LAG
 
             @pl.when(inside(q))
             def _():
@@ -443,19 +465,20 @@
             cold_pass_copy(False).wait_recv()
             build_cold()
 
-        @pl.when(tick + early < CHUNKS)
+        @pl.when(tick + EARLY < CHUNKS)
         def _():
-            og_copy(tick + early).start()
+            og_copy(tick + EARLY).start()
 
         @pl.when(tick < CHUNKS)
         def _():
             products(tick)
 
-        q = tick - COLD_LAG
-
-        @pl.when(inside(q))
-        def _():
-            cold_products(q)
+        for e in range(2):
+            q = 2 * (tick - COLD_LAG) + e
+
+            @pl.when(inside(q))
+            def _():
+                cold_products(q)
 
     for k in range(1, n_t):
         sel_copy(0, k).wait_send()
@@ -479,7 +502,7 @@
                 def _():
                     hot_copy(up, d, q).wait_send()
 
-                @pl.when(t == n_t - 1 if up else t == 0)
+                @pl.when(waits_late(up, d))
                 def _():
                     hot_copy(up, d, q).wait_recv()
 
@@ -539,7 +562,7 @@
             dma((2, n_t, CHUNKS)),
         ],
         compiler_params=pltpu.CompilerParams(
-            collective_id=0, has_side_effects=True, vmem_limit_bytes=42 * 1024 * 1024
+            collective_id=0, has_side_effects=True, vmem_limit_bytes=34 * 1024 * 1024
         ),
     )(owner_t, outbox, cold_outbox, out_grad, master, moment, second)
 
@@ -584,7 +607,7 @@
         in_specs=[vmem] * 5,
         out_specs=[hbm] * 5,
         scratch_shapes=[pltpu.SemaphoreType.DMA((4 + n_t, CHUNKS))],
-        compiler_params=pltpu.CompilerParams(vmem_limit_bytes=40 * 1024 * 1024),
+        compiler_params=pltpu.CompilerParams(vmem_limit_bytes=2 * 1024 * 1024),
     )(*parts)
 
 

time: 140 us -> 124 us (0.89)
  Pallas kernels: 134 us -> 122 us
  local copies, waits for them, and re-layouts: 4.83 us -> 0.01 us
    pallas_call x1, Pallas kernels: 120 us -> 112 us  [exchange(): pl.pallas_call(functools.partial(exchange_kernel, n_dp, n_t), out_shape=(...]
    unnamed x6 -> x2, local copies, waits for them, and re-layouts: 4.83 us -> 0.01 us
    pallas_call x1, Pallas kernels: 10.9 us -> 7.51 us  [place_out(): pl.pallas_call(functools.partial(place_kernel, n_t), out_shape=(jax.Shape...]
where the time goes in v3:
time: 124 us; the launch traced here: 123 us
  Pallas kernels  122 us (98%)
    pallas_call x1, Pallas kernels, exchange(): pl.pallas_call(functools.partial(exchange_kernel, n_dp, n_t), out_shape=(...  112 us
    pallas_call x1, Pallas kernels, place_out(): pl.pallas_call(functools.partial(place_kernel, n_t), out_shape=(jax.Shape...  7.51 us
    pallas_call x1, Pallas kernels, gather(): pl.pallas_call(functools.partial(gather_kernel, n_dp, n_t, unit), out_sha...  2.6 us

profile of v3, /device:TPU:1, one launch (start us, length us, event | category | flops | bytes accessed | tf_op | source)
XLA Modules:
  0.0 122.7 jit_solution(13551436802403339263)
XLA Ops:
  0.6 0.0 copy-start
  0.6 2.6 %shard_map.110 = (bf16[2,4,96,512]{3,2,1,0:T(8,128)(2,1)S(1)}, bf16[4,96,512]{2,1,0:T(8,128)(2,1)S(1)}) custom-call(s32[4,12]{1,0:T(4,128)} %ids_ref.1, s32[4,8]{1,0:T(4,128)} %bitcast.1, bf16[96,16384]{1,0:T(8,128)(2,1)} %act.1), custom_call_target="tpu_custom_call" | custom-call | tf_op jit(solution)/shard_map/pallas_call | solution.py:105
  3.3 0.0 copy-done
  3.3 111.9 %shard_map.111 = (f32[16,128,256]{2,1,0:T(8,128)S(1)}, f32[16,128,256]{2,1,0:T(8,128)S(1)}, f32[16,128,256]{2,1,0:T(8,128)S(1)}, bf16[4,16,128,256]{3,2,1,0:T(8,128)(2,1)S(1)}, f32[16,512,256]{2,1,0:T(8,128)S(1)}) custom-call(s32[4,8]{1,0:T(4,128)S(1)} %bitcast.2, bf16[2,4,96,512]{3,2,1,0:T(8,128)(2,1)S(1)} %get-tuple-element.12.outbox, ...), custom_call_target="tpu_custom_call" | custom-call | tf_op jit(solution)/shard_map/pallas_call | solution.py:523
  115.1 7.5 %shard_map.112 = (f32[128,4096]{1,0:T(8,128)}, f32[128,4096]{1,0:T(8,128)}, f32[128,4096]{1,0:T(8,128)}, bf16[128,16384]{1,0:T(8,128)(2,1)}, f32[512,4096]{1,0:T(8,128)}) custom-call(f32[16,128,256]{2,1,0:T(8,128)S(1)} %get-tuple-element.14.master, f32[16,128,256]{2,1,0:T(8,128)S(1)} %get-tuple-element.15.moment, ...), custom_call_target="tpu_custom_call" | custom-call | tf_op jit(solution)/shard_map/pallas_call | solution.py:598
Async XLA Ops:
  0.6 2.6 %copy-start = (s32[8,4]{0,1:T(4,128)S(1)}, s32[8,4]{0,1:T(4,128)}, u32[]{:S(2)}) copy-start(s32[8,4]{0,1:T(4,128)} %param.10) | copy-start | bytes 388

commit v4 on v3

v4 whole, which is shorter than its diff:
```python
import functools

import jax
import jax.numpy as jnp
from jax import lax
from jax.experimental import pallas as pl
from jax.experimental.pallas import tpu as pltpu
from jax.sharding import PartitionSpec as P

BLOCK = 128
HOT = 8
COLD = 4
MOSTC = 3

BETA_ONE = 0.9
BETA_TWO = 0.95
ADAM_EPS = 1e-08
LEARN_RATE = 0.01
DECAY = 0.1
CORRECT_ONE = 1.0 - 0.9**10
CORRECT_TWO = 1.0 - 0.95**10

CHUNKS = 16
FIRST = 4
EARLY = 4
MERGE_LAG = 1
SETTLE_LAG = 3
RELAY_LAG = 2
REACH = 2
COLD_STEP = 4
MESH = pl.DeviceIdType.MESH
F32 = jnp.float32
BF16 = jnp.bfloat16


def adam(grad, master, moment, second):
    new_moment = BETA_ONE * moment + (1.0 - BETA_ONE) * grad
    new_second = BETA_TWO * second + (1.0 - BETA_TWO) * grad * grad
    update = new_moment / CORRECT_ONE / (jnp.sqrt(new_second / CORRECT_TWO) + ADAM_EPS)
    return master - LEARN_RATE * (update + DECAY * master), new_moment, new_second


def phase_bit(n_dp, unit):
    return 1 if unit % BLOCK == 0 else 4


def free_bits(n_dp, unit):
    return [b for b in (1 << k for k in range(n_dp.bit_length() - 1)) if b not in (2, phase_bit(n_dp, unit))]


def flip(d, bit):
    return d + bit - 2 * bit * ((d // bit) % 2)


def phase_block(n_dp, unit, side, phase, col):
    place = col // unit
    d = side * 2 + phase * phase_bit(n_dp, unit)
    for k, b in enumerate(free_bits(n_dp, unit)):
        d = d + ((place >> k) % 2) * b
    return (d * unit + col % unit) // BLOCK


def exchange_kernel(
    n_dp,
    n_t,
    ids_ref,
    owner_ref,
    act_hbm,
    og_hbm,
    master_hbm,
    moment_hbm,
    second_hbm,
    master,
    moment,
    second,
    hot,
    cold,
    act,
    outbox,
    cold_outbox,
    inbox,
    cold_inbox,
    part_inbox,
    part_cold,
    peer_cold,
    og,
    flat,
    lhs,
    cold_lhs,
    acc,
    rs_send,
    rs_recv,
    og_load_sem,
    load_sem,
    sel_send_sem,
    sel_recv_sem,
    pass_send_sem,
    pass_recv_sem,
    cold_send_sem,
    cold_recv_sem,
    peer_send_sem,
    peer_recv_sem,
    og_send_sem,
    og_recv_sem,
    rs_send_sem,
    rs_recv_sem,
    hot_send_sem,
    hot_recv_sem,
    act_sem,
):
    i = lax.axis_index("dp")
    t = lax.axis_index("tensor")
    odd = i % 2
    peer = flip(i, 1)
    nxt, prv = (i + 1) % n_dp, (i + n_dp - 1) % n_dp
    part = (i + n_dp + 2 * odd - 1) % n_dp
    unit = master.shape[1]
    free = free_bits(n_dp, unit)
    bits = [phase_bit(n_dp, unit)] + free
    my_phase = (i // bits[0]) % 2
    stages = len(bits)
    units = n_dp // 4
    rows_tok = cold_outbox.shape[1]
    tok = og.shape[1] // 3
    chunk = og.shape[2]

    blocks = act.shape[0]

    def act_load(b):
        cols = pl.ds(pl.multiple_of(b * BLOCK, BLOCK), BLOCK)
        return pltpu.make_async_copy(act_hbm.at[:, cols], act.at[b], act_sem)

    @pl.loop(0, blocks)
    def _(b):
        act_load(b).start()

    def cut(ref, q):
        return ref.at[:, pl.ds(pl.multiple_of(q * chunk, chunk), chunk)]

    def og_load(q):
        return pltpu.make_async_copy(
            cut(og_hbm, q), og.at[q, pl.ds(0, tok)], og_load_sem.at[q]
        )

    @pl.loop(0, CHUNKS)
    def _(q):
        og_load(q).start()

    def state_load(which, q):
        source = (master_hbm, moment_hbm, second_hbm)[which]
        target = (master, moment, second)[which]
        return pltpu.make_async_copy(cut(source, q), target.at[q], load_sem.at[which, q])

    partners = [(flip(i, b), t) for b in bits] + [(part, t)]
    partners += [(i, (t + k) % n_t) for k in range(1, n_t)]
    barrier = pltpu.get_barrier_semaphore()
    for partner in partners:
        pl.semaphore_signal(barrier, inc=1, device_id=partner, device_id_type=MESH)

    owned = [owner_ref[c, i] for c in range(COLD)]
    ones = owned[0]
    for c in range(1, COLD):
        ones = ones + owned[c]
    place, taken, left = [], 0, ones
    for c in range(COLD):
        place.append(owned[c] * taken + (1 - owned[c]) * left)
        taken, left = taken + owned[c], left + 1 - owned[c]
    side = (i // 2) % 2

    def pick(phase, which):
        for k in range(n_t):
            group = (t + k) % n_t
            for b in range(outbox.shape[4] // BLOCK):
                index = phase_block(n_dp, unit, (side + which) % 2, phase, b * BLOCK)
                cols = act[ids_ref[group, index]]
                lanes = pl.ds(b * BLOCK, BLOCK)
                if k == 0:
                    inbox[which, phase, mine, lanes] = cols
                else:
                    outbox[which, phase, k, :, lanes] = cols

    def pick_cold():
        for k in range(n_t):
            group = (t + k) % n_t
            for p in range(COLD):
                block = 0
                for c in range(COLD):
                    block = block + jnp.where(place[c] == p, ids_ref[group, HOT + c], 0)
                lanes = pl.ds(p * BLOCK, BLOCK)
                if k == 0:
                    cold_inbox[mine, lanes] = act[block]
                else:
                    cold_outbox[k, :, lanes] = act[block]

    mine = pl.ds(t * rows_tok, rows_tok)

    def sel_copy(which, phase, k):
        return pltpu.make_async_remote_copy(
            src_ref=outbox.at[which, phase, k],
            dst_ref=inbox.at[which, phase, mine],
            send_sem=sel_send_sem.at[which + 2 * phase, k],
            recv_sem=sel_recv_sem.at[which + 2 * phase, k],
            device_id=(i, (t + k) % n_t),
            device_id_type=MESH,
        )

    def cold_sel_copy(k):
        return pltpu.make_async_remote_copy(
            src_ref=cold_outbox.at[k],
            dst_ref=cold_inbox.at[mine],
            send_sem=sel_send_sem.at[4, k],
            recv_sem=sel_recv_sem.at[4, k],
            device_id=(i, (t + k) % n_t),
            device_id_type=MESH,
        )

    def pass_copy(phase, k):
        rows = pl.ds(((t + n_t - k) % n_t) * rows_tok, rows_tok)
        return pltpu.make_async_remote_copy(
            src_ref=inbox.at[1, phase, rows],
            dst_ref=part_inbox.at[phase, rows],
            send_sem=pass_send_sem.at[phase, k],
            recv_sem=pass_recv_sem.at[phase, k],
            device_id=(part, t),
            device_id_type=MESH,
        )

    def og_copy(q):
        return pltpu.make_async_remote_copy(
            src_ref=og.at[q, pl.ds(0, tok)],
            dst_ref=og.at[q, pl.ds(tok, tok)],
            send_sem=og_send_sem.at[q],
            recv_sem=og_recv_sem.at[q],
            device_id=(part, t),
            device_id_type=MESH,
        )

    og_peer_copy = pltpu.make_async_remote_copy(
        src_ref=og.at[:, pl.ds(0, tok)],
        dst_ref=og.at[:, pl.ds(2 * tok, tok)],
        send_sem=peer_send_sem.at[0],
        recv_sem=peer_recv_sem.at[0],
        device_id=(peer, t),
        device_id_type=MESH,
    )

    @pl.loop(0, blocks)
    def _(b):
        act_load(b).wait()

    pick(0, 1)
    pl.semaphore_wait(barrier, len(partners))
    lower = t < n_t // 2
    far = [jnp.where(lower, k, n_t - k) for k in range(n_t - 1, 0, -1)]
    for k in far:
        sel_copy(1, 0, k).start()
    og_load(0).wait()
    og_copy(0).start()
    pass_copy(0, 0).start()
    for which, phase in ((0, 0), (1, 1), (0, 1)):
        pick(phase, which)
        for k in far:
            sel_copy(which, phase, k).start()
    pick_cold()
    for k in far:
        cold_sel_copy(k).start()

    @pl.loop(1, CHUNKS)
    def _(q):
        og_load(q).wait()

    og_peer_copy.start()

    @pl.loop(0, CHUNKS)
    def _(q):
        for which in range(3):
            state_load(which, q).start()

    og_copy(0).wait_recv()
    og_copy(1).start()
    def pass_on(phase):
        for k in far:
            sel_copy(1, phase, k).wait_recv()
            pass_copy(phase, k).start()

    pass_on(0)
    for q in range(2, EARLY):
        og_copy(q).start()

    def build_hot(phase, first, source):
        depth = pl.ds(first, tok)
        flat[:, depth] = source[...].T
        for r in range(units):
            place_ = 0
            for k, b in enumerate(free):
                bit = (i // b) % 2
                if r & (1 << (stages - 2 - k)):
                    bit = 1 - bit
                place_ = place_ + bit * (1 << k)
            rows = pl.ds(pl.multiple_of(place_ * unit, unit), unit)
            lhs[phase, pl.ds(r * unit, unit), depth] = flat[rows, depth]

    def receive_hot(phase):
        for k in far:
            sel_copy(0, phase, k).wait_recv()
        build_hot(phase, 0, inbox.at[0, phase])
        for k in range(n_t):
            pass_copy(phase, k).wait_recv()
        build_hot(phase, tok, part_inbox.at[phase])

    receive_hot(0)

    counts = [units >> s for s in range(stages)]
    offset = [sum(counts[:s]) * unit for s in range(stages)]

    def rs_copy(s, q):
        place_ = (q, pl.ds(offset[s], counts[s] * unit))
        return pltpu.make_async_remote_copy(
            src_ref=rs_send.at[place_],
            dst_ref=rs_recv.at[place_],
            send_sem=rs_send_sem.at[s, q],
            recv_sem=rs_recv_sem.at[s, q],
            device_id=(flip(i, bits[s]), t),
            device_id_type=MESH,
        )

    def hot_copy(up, d, q):
        step = d if d <= REACH else 1
        origin = t if d <= REACH else (t - (d - 1) if up else t + (d - 1))
        side = 0 if up else 1
        return pltpu.make_async_remote_copy(
            src_ref=hot.at[origin, q],
            dst_ref=hot.at[origin, q],
            send_sem=hot_send_sem.at[side, d, q],
            recv_sem=hot_recv_sem.at[side, d, q],
            device_id=(i, t + step if up else t - step),
            device_id_type=MESH,
        )

    def gets(up, d):
        return t >= d if up else t < n_t - d

    def sends(up, d):
        if d <= REACH:
            return t < n_t - d if up else t >= d
        return (t >= d - 1) & (t < n_t - 1) if up else (t <= n_t - d) & (t > 0)

    def waits_late(up, d):
        if d < REACH:
            return gets(up, d)
        return gets(up, d) & (t == n_t - 1 if up else t == 0)

    def cold_pass_copy(to_part):
        first = (1 - odd) if to_part else odd
        which = 0 if to_part else 1
        return pltpu.make_async_remote_copy(
            src_ref=cold_inbox.at[:, pl.ds(pl.multiple_of(first * BLOCK, BLOCK), MOSTC * BLOCK)],
            dst_ref=part_cold if to_part else peer_cold,
            send_sem=cold_send_sem.at[which],
            recv_sem=cold_recv_sem.at[which],
            device_id=(part if to_part else peer, t),
            device_id_type=MESH,
        )

    def ones_before(row, c):
        count = 0
        for b in range(c):
            count = count + owner_ref[b, row]
        return count

    def build_cold(place_, source, row, is_prev):
        slots = [source[:, pl.ds(p * BLOCK, BLOCK)].astype(F32) for p in range(MOSTC)]
        for c in range(COLD):
            before = ones_before(row, c)
            after = ones_before(row, COLD) + c - before - (COLD - MOSTC)
            slot = before * is_prev + after * (1 - is_prev)
            taken = jnp.where(owner_ref[c, row] == is_prev, 1.0, 0.0)
            cols = jnp.zeros((tok, BLOCK), F32)
            for p in range(MOSTC):
                cols = cols + slots[p] * (jnp.where(slot == p, 1.0, 0.0) * taken)
            cold_lhs[pl.ds(c * BLOCK, BLOCK), pl.ds(place_ * tok, tok)] = cols.astype(BF16).T

    def products(q, phase):
        @pl.when((q > 0) & (phase == 0))
        def _():
            og_copy(q).wait_recv()

        out = jnp.dot(lhs[phase], og[q, pl.ds(0, 2 * tok)], preferred_element_type=F32)

        @pl.when(my_phase == phase)
        def _():
            acc[q] = out

        @pl.when(my_phase != phase)
        def _():
            rs_send[q, pl.ds(0, units * unit)] = out.astype(BF16)
            rs_copy(0, q).start()

    def cold_products(q):
        cold[q] = jnp.dot(cold_lhs[...], og[q, pl.ds(tok, 2 * tok)], preferred_element_type=F32)

    def settle(s, q):
        rs_copy(s, q).wait_recv()
        held = counts[s] * unit
        got = rs_recv[q, pl.ds(offset[s], held)].astype(F32)
        total = acc[q, pl.ds(0, held)] + got
        if s < stages - 1:
            sent = counts[s + 1] * unit
            rs_send[q, pl.ds(offset[s + 1], sent)] = total[sent:].astype(BF16)
            rs_copy(s + 1, q).start()
            acc[q, pl.ds(0, sent)] = total[:sent]
            return
        for which in range(3):
            state_load(which, q).wait()

        new_master, new_moment, new_second = adam(total, master[q], moment[q], second[q])
        hot[t, q] = new_master.astype(BF16)
        for d in range(1, min(REACH + 1, n_t)):
            for up in (True, False):

                @pl.when(sends(up, d))
                def _():
                    hot_copy(up, d, q).start()

        master[q] = new_master
        moment[q] = new_moment
        second[q] = new_second

    def relay(up, d, q):
        @pl.when(sends(up, d + 1))
        def _():
            hot_copy(up, d, q).wait_recv()
            hot_copy(up, d + 1, q).start()

    def inside(q):
        return (q >= 0) & (q < CHUNKS)

    settled = MERGE_LAG + (stages - 1) * SETTLE_LAG
    works = 2 * CHUNKS
    cold_first = works + settled
    ticks = cold_first + max(max(n_t - 1 - REACH, 0) * RELAY_LAG, CHUNKS // COLD_STEP)

    def work(index):
        later = jnp.minimum(index // (2 * FIRST), 1)
        q = (1 - later) * (index % FIRST) + later * (index // 2)
        phase = (1 - later) * ((index // FIRST) % 2) + later * (index % 2)
        return q, phase

    def at(index, do):
        @pl.when((index >= 0) & (index < works))
        def _():
            do(*work(jnp.maximum(index, 0)))

    def owned_at(index, do):
        def when_owned(q, phase):
            @pl.when(phase == my_phase)
            def _():
                do(q)

        at(index, when_owned)

    @pl.loop(0, ticks)
    def _(tick):
        for s in reversed(range(stages)):
            owned_at(tick - MERGE_LAG - s * SETTLE_LAG, functools.partial(settle, s))

        def pass_along(d, q):
            relay(True, d, q)
            relay(False, d, q)

        for d in range(REACH, n_t - 1):
            back = settled + (d - REACH + 1) * RELAY_LAG
            owned_at(tick - back, functools.partial(pass_along, d))

        @pl.when(tick == cold_first - 1)
        def _():
            og_peer_copy.wait_recv()
            cold_pass_copy(False).wait_recv()
            build_cold(1, peer_cold, peer, odd)

        @pl.when(tick == cold_first)
        def _():
            cold_pass_copy(True).wait_recv()
            build_cold(0, part_cold, part, 1 - odd)

        @pl.when(tick == FIRST)
        def _():
            receive_hot(1)

        at(tick, products)

        @pl.when(tick == 0)
        def _():
            pass_copy(1, 0).start()
            pass_on(1)

        def feed(q, phase):
            @pl.when((phase == 0) & (q + EARLY < CHUNKS))
            def _():
                og_copy(q + EARLY).start()

            @pl.when((phase == 0) & (q + EARLY == CHUNKS - 1))
            def _():
                for k in far:
                    cold_sel_copy(k).wait_recv()
                cold_pass_copy(True).start()
                cold_pass_copy(False).start()

        at(tick, feed)

        for e in range(COLD_STEP):
            q = COLD_STEP * (tick - cold_first) + e

            @pl.when(inside(q))
            def _():
                cold_products(q)

    for k in range(1, n_t):
        for which in range(2):
            for phase in range(2):
                sel_copy(which, phase, k).wait_send()
        cold_sel_copy(k).wait_send()
    for k in range(n_t):
        pass_copy(0, k).wait_send()
        pass_copy(1, k).wait_send()
    og_peer_copy.wait_send()
    cold_pass_copy(True).wait_send()
    cold_pass_copy(False).wait_send()

    @pl.loop(0, CHUNKS)
    def _(q):
        og_copy(q).wait_send()
        for s in range(stages):
            rs_copy(s, q).wait_send()
        for d in range(1, n_t):
            for up in (True, False):

                @pl.when(sends(up, d))
                def _():
                    hot_copy(up, d, q).wait_send()

                @pl.when(waits_late(up, d))
                def _():
                    hot_copy(up, d, q).wait_recv()


def exchange(n_dp, n_t, ids, owner_t, activations, out_grad, master, moment, second):
    rows_tok, width = activations.shape
    tok, qlocal = out_grad.shape
    unit = master.shape[0]
    chunk = qlocal // CHUNKS
    units = n_dp // 4
    wide = units * unit
    stages = 1 + len(free_bits(n_dp, unit))
    traded = sum(units >> s for s in range(stages)) * unit
    smem = pl.BlockSpec(memory_space=pltpu.SMEM)
    vmem = pl.BlockSpec(memory_space=pltpu.VMEM)
    hbm = pl.BlockSpec(memory_space=pltpu.HBM)
    dma = pltpu.SemaphoreType.DMA
    return pl.pallas_call(
        functools.partial(exchange_kernel, n_dp, n_t),
        out_shape=(
            pltpu.VMEM((CHUNKS, unit, chunk), F32),
            pltpu.VMEM((CHUNKS, unit, chunk), F32),
            pltpu.VMEM((CHUNKS, unit, chunk), F32),
            pltpu.VMEM((n_t, CHUNKS, unit, chunk), BF16),
            pltpu.VMEM((CHUNKS, COLD * BLOCK, chunk), F32),
        ),
        in_specs=[smem, smem] + [hbm] * 5,
        out_specs=[vmem] * 5,
        scratch_shapes=[
            pltpu.VMEM((width // BLOCK, rows_tok, BLOCK), BF16),
            pltpu.VMEM((2, 2, n_t, rows_tok, wide), BF16),
            pltpu.VMEM((n_t, rows_tok, COLD * BLOCK), BF16),
            pltpu.VMEM((2, 2, tok, wide), BF16),
            pltpu.VMEM((tok, COLD * BLOCK), BF16),
            pltpu.VMEM((2, tok, wide), BF16),
            pltpu.VMEM((tok, MOSTC * BLOCK), BF16),
            pltpu.VMEM((tok, MOSTC * BLOCK), BF16),
            pltpu.VMEM((CHUNKS, 3 * tok, chunk), BF16),
            pltpu.VMEM((wide, 2 * tok), BF16),
            pltpu.VMEM((2, wide, 2 * tok), BF16),
            pltpu.VMEM((COLD * BLOCK, 2 * tok), BF16),
            pltpu.VMEM((CHUNKS, wide, chunk), F32),
            pltpu.VMEM((CHUNKS, traded, chunk), BF16),
            pltpu.VMEM((CHUNKS, traded, chunk), BF16),
            dma((CHUNKS,)),
            dma((3, CHUNKS)),
            dma((5, n_t)),
            dma((5, n_t)),
            dma((2, n_t)),
            dma((2, n_t)),
            dma((2,)),
            dma((2,)),
            dma((1,)),
            dma((1,)),
            dma((CHUNKS,)),
            dma((CHUNKS,)),
            dma((stages, CHUNKS)),
            dma((stages, CHUNKS)),
            dma((2, n_t, CHUNKS)),
            dma((2, n_t, CHUNKS)),
            dma(()),
        ],
        compiler_params=pltpu.CompilerParams(
            collective_id=0, has_side_effects=True, vmem_limit_bytes=40 * 1024 * 1024
        ),
    )(ids, owner_t, activations, out_grad, master, moment, second)


def place_kernel(n_t, master, moment, second, hot, cold, *refs):
    outs, sem = refs[:5], refs[5]
    chunk = master.shape[2]

    jobs = [(4, 0)] + [(w, 0) for w in range(3)] + [(3, g) for g in range(n_t)]

    def all_of(act):
        @pl.loop(0, CHUNKS)
        def _(q):
            for which, g in jobs:
                slot = which if which < 3 else (3 if which == 4 else 4 + g)
                source = (master, moment, second, hot.at[g], cold)[which]
                cols = pl.ds(pl.multiple_of((g * CHUNKS + q) * chunk, chunk), chunk)
                act(
                    pltpu.make_async_copy(
                        source.at[q], outs[which].at[:, cols], sem.at[slot, q]
                    )
                )

    all_of(lambda copy: copy.start())
    all_of(lambda copy: copy.wait())


def place_out(n_t, parts):
    chunks, unit, chunk = parts[0].shape
    qlocal = chunks * chunk
    vmem = pl.BlockSpec(memory_space=pltpu.VMEM)
    hbm = pl.BlockSpec(memory_space=pltpu.HBM)
    return pl.pallas_call(
        functools.partial(place_kernel, n_t),
        out_shape=(
            jax.ShapeDtypeStruct((unit, qlocal), F32),
            jax.ShapeDtypeStruct((unit, qlocal), F32),
            jax.ShapeDtypeStruct((unit, qlocal), F32),
            jax.ShapeDtypeStruct((unit, qlocal * n_t), BF16),
            jax.ShapeDtypeStruct((parts[4].shape[1], qlocal), F32),
        ),
        in_specs=[vmem] * 5,
        out_specs=[hbm] * 5,
        scratch_shapes=[pltpu.SemaphoreType.DMA((4 + n_t, CHUNKS))],
        compiler_params=pltpu.CompilerParams(vmem_limit_bytes=2 * 1024 * 1024),
    )(*parts)


def per_device(n_dp, n_t, activations, out_grad, block_ids, owner_map, master, moment, second):
    parts = exchange(
        n_dp, n_t, block_ids, owner_map.T, activations, out_grad, master, moment, second
    )
    return tuple(place_out(n_t, parts))


def solution(mesh):
    return jax.shard_map(
        functools.partial(per_device, mesh.shape["dp"], mesh.shape["tensor"]),
        mesh=mesh,
        in_specs=(
            P(("dp", "tensor"), None),
            P("dp", "tensor"),
            P(),
            P(),
            P("dp", "tensor"),
            P("dp", "tensor"),
            P("dp", "tensor"),
        ),
        out_specs=(
            P("dp", "tensor"),
            P("dp", "tensor"),
            P("dp", "tensor"),
            P("dp", None),
            P("dp", "tensor"),
        ),
        check_vma=False,
    )
```

time: 124 us -> 117 us (0.944)
  Pallas kernels: 122 us -> 116 us
    pallas_call x1, Pallas kernels: 112 us -> 108 us  [exchange(): pl.pallas_call(functools.partial(exchange_kernel, n_dp, n_t), out_shape=(...]
    pallas_call x1 -> x0, Pallas kernels: 2.6 us -> none  [gather(): pl.pallas_call(functools.partial(gather_kernel, n_dp, n_t, unit), out_sha...]
where the time goes in v4:
time: 117 us; the launch traced here: 116 us
  Pallas kernels  116 us (99%)
    pallas_call x1, Pallas kernels, exchange(): pl.pallas_call(functools.partial(exchange_kernel, n_dp, n_t), out_shape=(...  108 us
    pallas_call x1, Pallas kernels, place_out(): pl.pallas_call(functools.partial(place_kernel, n_t), out_shape=(jax.Shape...  7.51 us

profile of v4, /device:TPU:1, one launch (start us, length us, event | category | flops | bytes accessed | tf_op | source)
XLA Modules:
  0.0 116.3 jit_solution(467559241345277146)
XLA Ops:
  0.6 108.2 %shard_map.110 = (f32[16,128,256]{2,1,0:T(8,128)S(1)}, f32[16,128,256]{2,1,0:T(8,128)S(1)}, f32[16,128,256]{2,1,0:T(8,128)S(1)}, bf16[4,16,128,256]{3,2,1,0:T(8,128)(2,1)S(1)}, f32[16,512,256]{2,1,0:T(8,128)S(1)}) custom-call(s32[4,12]{1,0:T(4,128)} %ids_ref.1, s32[4,8]{1,0:T(4,128)} %bitcast.1, bf16[96,16384]{1,0:T(8,128)(2,1)} %act_hbm.1, ...), custom_call_target="tpu_custom_call" | custom-call | tf_op jit(solution)/shard_map/pallas_call | solution.py:560
  108.8 7.5 %shard_map.111 = (f32[128,4096]{1,0:T(8,128)}, f32[128,4096]{1,0:T(8,128)}, f32[128,4096]{1,0:T(8,128)}, bf16[128,16384]{1,0:T(8,128)(2,1)}, f32[512,4096]{1,0:T(8,128)}) custom-call(f32[16,128,256]{2,1,0:T(8,128)S(1)} %get-tuple-element.10.master, f32[16,128,256]{2,1,0:T(8,128)S(1)} %get-tuple-element.11.moment, ...), custom_call_target="tpu_custom_call" | custom-call | tf_op jit(solution)/shard_map/pallas_call | solution.py:639

commit v5 on v4

--- a/solution.py
+++ b/solution.py
@@ -26,7 +26,6 @@
 MERGE_LAG = 1
 SETTLE_LAG = 3
 RELAY_LAG = 2
-REACH = 2
 COLD_STEP = 4
 MESH = pl.DeviceIdType.MESH
 F32 = jnp.float32
@@ -139,7 +138,7 @@
 
     def og_load(q):
         return pltpu.make_async_copy(
-            cut(og_hbm, q), og.at[q, pl.ds(0, tok)], og_load_sem.at[q]
+            cut(og_hbm, q), og.at[q, pl.ds(0, tok)], og_load_sem
         )
 
     @pl.loop(0, CHUNKS)
@@ -149,7 +148,7 @@
     def state_load(which, q):
         source = (master_hbm, moment_hbm, second_hbm)[which]
         target = (master, moment, second)[which]
-        return pltpu.make_async_copy(cut(source, q), target.at[q], load_sem.at[which, q])
+        return pltpu.make_async_copy(cut(source, q), target.at[q], load_sem)
 
     partners = [(flip(i, b), t) for b in bits] + [(part, t)]
     partners += [(i, (t + k) % n_t) for k in range(1, n_t)]
@@ -198,7 +197,7 @@
         return pltpu.make_async_remote_copy(
             src_ref=outbox.at[which, phase, k],
             dst_ref=inbox.at[which, phase, mine],
-            send_sem=sel_send_sem.at[which + 2 * phase, k],
+            send_sem=sel_send_sem,
             recv_sem=sel_recv_sem.at[which + 2 * phase, k],
             device_id=(i, (t + k) % n_t),
             device_id_type=MESH,
@@ -208,7 +207,7 @@
         return pltpu.make_async_remote_copy(
             src_ref=cold_outbox.at[k],
             dst_ref=cold_inbox.at[mine],
-            send_sem=sel_send_sem.at[4, k],
+            send_sem=sel_send_sem,
             recv_sem=sel_recv_sem.at[4, k],
             device_id=(i, (t + k) % n_t),
             device_id_type=MESH,
@@ -219,7 +218,7 @@
         return pltpu.make_async_remote_copy(
             src_ref=inbox.at[1, phase, rows],
             dst_ref=part_inbox.at[phase, rows],
-            send_sem=pass_send_sem.at[phase, k],
+            send_sem=pass_send_sem,
             recv_sem=pass_recv_sem.at[phase, k],
             device_id=(part, t),
             device_id_type=MESH,
@@ -229,7 +228,7 @@
         return pltpu.make_async_remote_copy(
             src_ref=og.at[q, pl.ds(0, tok)],
             dst_ref=og.at[q, pl.ds(tok, tok)],
-            send_sem=og_send_sem.at[q],
+            send_sem=og_send_sem,
             recv_sem=og_recv_sem.at[q],
             device_id=(part, t),
             device_id_type=MESH,
@@ -254,9 +253,13 @@
     far = [jnp.where(lower, k, n_t - k) for k in range(n_t - 1, 0, -1)]
     for k in far:
         sel_copy(1, 0, k).start()
-    og_load(0).wait()
+    @pl.loop(0, CHUNKS)
+    def _(q):
+        og_load(q).wait()
+
     og_copy(0).start()
     pass_copy(0, 0).start()
+    og_copy(1).start()
     for which, phase in ((0, 0), (1, 1), (0, 1)):
         pick(phase, which)
         for k in far:
@@ -265,10 +268,6 @@
     for k in far:
         cold_sel_copy(k).start()
 
-    @pl.loop(1, CHUNKS)
-    def _(q):
-        og_load(q).wait()
-
     og_peer_copy.start()
 
     @pl.loop(0, CHUNKS)
@@ -276,8 +275,6 @@
         for which in range(3):
             state_load(which, q).start()
 
-    og_copy(0).wait_recv()
-    og_copy(1).start()
     def pass_on(phase):
         for k in far:
             sel_copy(1, phase, k).wait_recv()
@@ -310,6 +307,11 @@
 
     receive_hot(0)
 
+    @pl.loop(0, CHUNKS)
+    def _(q):
+        for which in range(3):
+            state_load(which, q).wait()
+
     counts = [units >> s for s in range(stages)]
     offset = [sum(counts[:s]) * unit for s in range(stages)]
 
@@ -318,21 +320,22 @@
         return pltpu.make_async_remote_copy(
             src_ref=rs_send.at[place_],
             dst_ref=rs_recv.at[place_],
-            send_sem=rs_send_sem.at[s, q],
+            send_sem=rs_send_sem,
             recv_sem=rs_recv_sem.at[s, q],
             device_id=(flip(i, bits[s]), t),
             device_id_type=MESH,
         )
 
-    def hot_copy(up, d, q):
-        step = d if d <= REACH else 1
-        origin = t if d <= REACH else (t - (d - 1) if up else t + (d - 1))
+    def hot_copy(up, d, q, direct):
+        step = d if direct else 1
+        back = 0 if direct else d - 1
+        origin = t - back if up else t + back
         side = 0 if up else 1
         return pltpu.make_async_remote_copy(
             src_ref=hot.at[origin, q],
             dst_ref=hot.at[origin, q],
-            send_sem=hot_send_sem.at[side, d, q],
-            recv_sem=hot_recv_sem.at[side, d, q],
+            send_sem=hot_send_sem,
+            recv_sem=hot_recv_sem.at[side, d - 1, q],
             device_id=(i, t + step if up else t - step),
             device_id_type=MESH,
         )
@@ -341,14 +344,20 @@
         return t >= d if up else t < n_t - d
 
     def sends(up, d):
-        if d <= REACH:
-            return t < n_t - d if up else t >= d
-        return (t >= d - 1) & (t < n_t - 1) if up else (t <= n_t - d) & (t > 0)
+        if d == 1:
+            return t < n_t - 1 if up else t > 0
+        return t + d < n_t - 1 if up else t - d > 0
+
+    def passes(up, d):
+        if d == 1:
+            return (t == n_t - 2) & (t >= 1) if up else (t == 1) & (t < n_t - 1)
+        return (t >= d) & (t < n_t - 1) if up else (t < n_t - d) & (t > 0)
 
     def waits_late(up, d):
-        if d < REACH:
-            return gets(up, d)
-        return gets(up, d) & (t == n_t - 1 if up else t == 0)
+        late = t == n_t - 1 if up else t == 0
+        if d == 1:
+            late = late | ((t < n_t - 2) | (t < 1) if up else (t > 1) | (t == n_t - 1))
+        return gets(up, d) & late
 
     def cold_pass_copy(to_part):
         first = (1 - odd) if to_part else odd
@@ -381,7 +390,7 @@
             cold_lhs[pl.ds(c * BLOCK, BLOCK), pl.ds(place_ * tok, tok)] = cols.astype(BF16).T
 
     def products(q, phase):
-        @pl.when((q > 0) & (phase == 0))
+        @pl.when(phase == 0)
         def _():
             og_copy(q).wait_recv()
 
@@ -410,27 +419,24 @@
             rs_copy(s + 1, q).start()
             acc[q, pl.ds(0, sent)] = total[:sent]
             return
-        for which in range(3):
-            state_load(which, q).wait()
-
         new_master, new_moment, new_second = adam(total, master[q], moment[q], second[q])
         hot[t, q] = new_master.astype(BF16)
-        for d in range(1, min(REACH + 1, n_t)):
+        for d in reversed(range(1, min(3, n_t))):
             for up in (True, False):
 
                 @pl.when(sends(up, d))
                 def _():
-                    hot_copy(up, d, q).start()
+                    hot_copy(up, d, q, True).start()
 
         master[q] = new_master
         moment[q] = new_moment
         second[q] = new_second
 
     def relay(up, d, q):
-        @pl.when(sends(up, d + 1))
-        def _():
-            hot_copy(up, d, q).wait_recv()
-            hot_copy(up, d + 1, q).start()
+        @pl.when(passes(up, d))
+        def _():
+            hot_copy(up, d, q, True).wait_recv()
+            hot_copy(up, d + 1, q, False).start()
 
     def inside(q):
         return (q >= 0) & (q < CHUNKS)
@@ -438,7 +444,7 @@
     settled = MERGE_LAG + (stages - 1) * SETTLE_LAG
     works = 2 * CHUNKS
     cold_first = works + settled
-    ticks = cold_first + max(max(n_t - 1 - REACH, 0) * RELAY_LAG, CHUNKS // COLD_STEP)
+    ticks = cold_first + max((n_t - 2) * RELAY_LAG, CHUNKS // COLD_STEP)
 
     def work(index):
         later = jnp.minimum(index // (2 * FIRST), 1)
@@ -468,8 +474,8 @@
             relay(True, d, q)
             relay(False, d, q)
 
-        for d in range(REACH, n_t - 1):
-            back = settled + (d - REACH + 1) * RELAY_LAG
+        for d in range(1, n_t - 1):
+            back = settled + max(d - 1, 1) * RELAY_LAG
             owned_at(tick - back, functools.partial(pass_along, d))
 
         @pl.when(tick == cold_first - 1)
@@ -535,13 +541,16 @@
         for d in range(1, n_t):
             for up in (True, False):
 
-                @pl.when(sends(up, d))
+                sent = passes(up, d - 1) if d > 1 else t < 0
+                sent = sent | sends(up, d) if d < 3 else sent
+
+                @pl.when(sent)
                 def _():
-                    hot_copy(up, d, q).wait_send()
+                    hot_copy(up, d, q, True).wait_send()
 
                 @pl.when(waits_late(up, d))
                 def _():
-                    hot_copy(up, d, q).wait_recv()
+                    hot_copy(up, d, q, True).wait_recv()
 
 
 def exchange(n_dp, n_t, ids, owner_t, activations, out_grad, master, moment, second):
@@ -584,22 +593,22 @@
             pltpu.VMEM((CHUNKS, wide, chunk), F32),
             pltpu.VMEM((CHUNKS, traded, chunk), BF16),
             pltpu.VMEM((CHUNKS, traded, chunk), BF16),
-            dma((CHUNKS,)),
-            dma((3, CHUNKS)),
+            dma(()),
+            dma(()),
+            dma(()),
             dma((5, n_t)),
-            dma((5, n_t)),
-            dma((2, n_t)),
+            dma(()),
             dma((2, n_t)),
             dma((2,)),
             dma((2,)),
             dma((1,)),
             dma((1,)),
+            dma(()),
             dma((CHUNKS,)),
-            dma((CHUNKS,)),
+            dma(()),
             dma((stages, CHUNKS)),
-            dma((stages, CHUNKS)),
-            dma((2, n_t, CHUNKS)),
-            dma((2, n_t, CHUNKS)),
+            dma(()),
+            dma((2, n_t - 1, CHUNKS)),
             dma(()),
         ],
         compiler_params=pltpu.CompilerParams(
@@ -618,14 +627,9 @@
         @pl.loop(0, CHUNKS)
         def _(q):
             for which, g in jobs:
-                slot = which if which < 3 else (3 if which == 4 else 4 + g)
                 source = (master, moment, second, hot.at[g], cold)[which]
                 cols = pl.ds(pl.multiple_of((g * CHUNKS + q) * chunk, chunk), chunk)
-                act(
-                    pltpu.make_async_copy(
-                        source.at[q], outs[which].at[:, cols], sem.at[slot, q]
-                    )
-                )
+                act(pltpu.make_async_copy(source.at[q], outs[which].at[:, cols], sem))
 
     all_of(lambda copy: copy.start())
     all_of(lambda copy: copy.wait())
@@ -647,7 +651,7 @@
         ),
         in_specs=[vmem] * 5,
         out_specs=[hbm] * 5,
-        scratch_shapes=[pltpu.SemaphoreType.DMA((4 + n_t, CHUNKS))],
+        scratch_shapes=[pltpu.SemaphoreType.DMA],
         compiler_params=pltpu.CompilerParams(vmem_limit_bytes=2 * 1024 * 1024),
     )(*parts)
 

time: 117 us -> 113 us (0.966)
  Pallas kernels: 116 us -> 112 us
    pallas_call x1, Pallas kernels: 108 us -> 105 us  [exchange(): pl.pallas_call(functools.partial(exchange_kernel, n_dp, n_t), out_shape=(...]
where the time goes in v5:
time: 113 us; the launch traced here: 112 us
  Pallas kernels  112 us (99%)
    pallas_call x1, Pallas kernels, exchange(): pl.pallas_call(functools.partial(exchange_kernel, n_dp, n_t), out_shape=(...  105 us
    pallas_call x1, Pallas kernels, place_out(): pl.pallas_call(functools.partial(place_kernel, n_t), out_shape=(jax.Shape...  6.37 us

profile of v5, /device:TPU:1, one launch (start us, length us, event | category | flops | bytes accessed | tf_op | source)
XLA Modules:
  0.0 112.4 jit_solution(14239310548077917129)
XLA Ops:
  0.6 105.3 %shard_map.110 = (f32[16,128,256]{2,1,0:T(8,128)S(1)}, f32[16,128,256]{2,1,0:T(8,128)S(1)}, f32[16,128,256]{2,1,0:T(8,128)S(1)}, bf16[4,16,128,256]{3,2,1,0:T(8,128)(2,1)S(1)}, f32[16,512,256]{2,1,0:T(8,128)S(1)}) custom-call(s32[4,12]{1,0:T(4,128)} %ids_ref.1, s32[4,8]{1,0:T(4,128)} %bitcast.1, bf16[96,16384]{1,0:T(8,128)(2,1)} %act_hbm.1, ...), custom_call_target="tpu_custom_call" | custom-call | tf_op jit(solution)/shard_map/pallas_call | solution.py:569
  106.0 6.4 %shard_map.111 = (f32[128,4096]{1,0:T(8,128)}, f32[128,4096]{1,0:T(8,128)}, f32[128,4096]{1,0:T(8,128)}, bf16[128,16384]{1,0:T(8,128)(2,1)}, f32[512,4096]{1,0:T(8,128)}) custom-call(f32[16,128,256]{2,1,0:T(8,128)S(1)} %get-tuple-element.10.master, f32[16,128,256]{2,1,0:T(8,128)S(1)} %get-tuple-element.11.moment, ...), custom_call_target="tpu_custom_call" | custom-call | tf_op jit(solution)/shard_map/pallas_call | solution.py:643

commit v6 on v5

--- a/solution.py
+++ b/solution.py
@@ -21,6 +21,7 @@
 CORRECT_TWO = 1.0 - 0.95**10
 
 CHUNKS = 16
+STRIDE = 8
 FIRST = 4
 EARLY = 4
 MERGE_LAG = 1
@@ -123,38 +124,39 @@
     tok = og.shape[1] // 3
     chunk = og.shape[2]
 
-    blocks = act.shape[0]
-
-    def act_load(b):
-        cols = pl.ds(pl.multiple_of(b * BLOCK, BLOCK), BLOCK)
-        return pltpu.make_async_copy(act_hbm.at[:, cols], act.at[b], act_sem)
-
-    @pl.loop(0, blocks)
-    def _(b):
-        act_load(b).start()
-
-    def cut(ref, q):
-        return ref.at[:, pl.ds(pl.multiple_of(q * chunk, chunk), chunk)]
-
-    def og_load(q):
-        return pltpu.make_async_copy(
-            cut(og_hbm, q), og.at[q, pl.ds(0, tok)], og_load_sem
-        )
-
-    @pl.loop(0, CHUNKS)
-    def _(q):
-        og_load(q).start()
-
-    def state_load(which, q):
-        source = (master_hbm, moment_hbm, second_hbm)[which]
-        target = (master, moment, second)[which]
-        return pltpu.make_async_copy(cut(source, q), target.at[q], load_sem)
-
     partners = [(flip(i, b), t) for b in bits] + [(part, t)]
     partners += [(i, (t + k) % n_t) for k in range(1, n_t)]
     barrier = pltpu.get_barrier_semaphore()
     for partner in partners:
         pl.semaphore_signal(barrier, inc=1, device_id=partner, device_id_type=MESH)
+
+    blocks = act.shape[0]
+
+    def act_load(b):
+        cols = pl.ds(pl.multiple_of(b * BLOCK, BLOCK), BLOCK)
+        return pltpu.make_async_copy(act_hbm.at[:, cols], act.at[b], act_sem)
+
+    @pl.loop(0, blocks // STRIDE)
+    def _(b):
+        for e in range(STRIDE):
+            act_load(b * STRIDE + e).start()
+
+    def cut(ref, q):
+        return ref.at[:, pl.ds(pl.multiple_of(q * chunk, chunk), chunk)]
+
+    def og_load(q):
+        return pltpu.make_async_copy(
+            cut(og_hbm, q), og.at[q, pl.ds(0, tok)], og_load_sem
+        )
+
+    @pl.loop(0, CHUNKS)
+    def _(q):
+        og_load(q).start()
+
+    def state_load(which, q):
+        source = (master_hbm, moment_hbm, second_hbm)[which]
+        target = (master, moment, second)[which]
+        return pltpu.make_async_copy(cut(source, q), target.at[q], load_sem)
 
     owned = [owner_ref[c, i] for c in range(COLD)]
     ones = owned[0]
@@ -243,9 +245,10 @@
         device_id_type=MESH,
     )
 
-    @pl.loop(0, blocks)
+    @pl.loop(0, blocks // STRIDE)
     def _(b):
-        act_load(b).wait()
+        for e in range(STRIDE):
+            act_load(b * STRIDE + e).wait()
 
     pick(0, 1)
     pl.semaphore_wait(barrier, len(partners))
@@ -253,6 +256,7 @@
     far = [jnp.where(lower, k, n_t - k) for k in range(n_t - 1, 0, -1)]
     for k in far:
         sel_copy(1, 0, k).start()
+
     @pl.loop(0, CHUNKS)
     def _(q):
         og_load(q).wait()
@@ -307,11 +311,6 @@
 
     receive_hot(0)
 
-    @pl.loop(0, CHUNKS)
-    def _(q):
-        for which in range(3):
-            state_load(which, q).wait()
-
     counts = [units >> s for s in range(stages)]
     offset = [sum(counts[:s]) * unit for s in range(stages)]
 
@@ -330,13 +329,23 @@
         step = d if direct else 1
         back = 0 if direct else d - 1
         origin = t - back if up else t + back
-        side = 0 if up else 1
         return pltpu.make_async_remote_copy(
             src_ref=hot.at[origin, q],
             dst_ref=hot.at[origin, q],
             send_sem=hot_send_sem,
-            recv_sem=hot_recv_sem.at[side, d - 1, q],
+            recv_sem=hot_recv_sem.at[origin, q],
             device_id=(i, t + step if up else t - step),
+            device_id_type=MESH,
+        )
+
+    def arrival(up, d, q):
+        origin = t - d if up else t + d
+        return pltpu.make_async_remote_copy(
+            src_ref=hot.at[origin, q],
+            dst_ref=hot.at[origin, q],
+            send_sem=hot_send_sem,
+            recv_sem=hot_recv_sem.at[origin, q],
+            device_id=(i, origin),
             device_id_type=MESH,
         )
 
@@ -435,7 +444,7 @@
     def relay(up, d, q):
         @pl.when(passes(up, d))
         def _():
-            hot_copy(up, d, q, True).wait_recv()
+            arrival(up, d, q).wait_recv()
             hot_copy(up, d + 1, q, False).start()
 
     def inside(q):
@@ -492,6 +501,13 @@
         @pl.when(tick == FIRST)
         def _():
             receive_hot(1)
+
+        @pl.when(tick == 1)
+        def _():
+            @pl.loop(0, CHUNKS)
+            def _(q):
+                for which in range(3):
+                    state_load(which, q).wait()
 
         at(tick, products)
 
@@ -550,7 +566,7 @@
 
                 @pl.when(waits_late(up, d))
                 def _():
-                    hot_copy(up, d, q, True).wait_recv()
+                    arrival(up, d, q).wait_recv()
 
 
 def exchange(n_dp, n_t, ids, owner_t, activations, out_grad, master, moment, second):
@@ -608,7 +624,7 @@
             dma(()),
             dma((stages, CHUNKS)),
             dma(()),
-            dma((2, n_t - 1, CHUNKS)),
+            dma((n_t, CHUNKS)),
             dma(()),
         ],
         compiler_params=pltpu.CompilerParams(

time: 113 us -> 112 us (level)
  no operation moved by 1% of the time
where the time goes in v6:
time: 112 us
  Pallas kernels  111 us (99%)
    pallas_call x1, Pallas kernels, exchange(): pl.pallas_call(functools.partial(exchange_kernel, n_dp, n_t), out_shape=(...  105 us
    pallas_call x1, Pallas kernels, place_out(): pl.pallas_call(functools.partial(place_kernel, n_t), out_shape=(jax.Shape...  6.37 us

profile of v6, /device:TPU:1, one launch (start us, length us, event | category | flops | bytes accessed | tf_op | source)
XLA Modules:
  0.0 111.5 jit_solution(9381033701106254795)
XLA Ops:
  0.6 104.5 %shard_map.110 = (f32[16,128,256]{2,1,0:T(8,128)S(1)}, f32[16,128,256]{2,1,0:T(8,128)S(1)}, f32[16,128,256]{2,1,0:T(8,128)S(1)}, bf16[4,16,128,256]{3,2,1,0:T(8,128)(2,1)S(1)}, f32[16,512,256]{2,1,0:T(8,128)S(1)}) custom-call(s32[4,12]{1,0:T(4,128)} %ids_ref.1, s32[4,8]{1,0:T(4,128)} %bitcast.1, bf16[96,16384]{1,0:T(8,128)(2,1)} %act_hbm.1, ...), custom_call_target="tpu_custom_call" | custom-call | tf_op jit(solution)/shard_map/pallas_call | solution.py:585
  105.2 6.4 %shard_map.111 = (f32[128,4096]{1,0:T(8,128)}, f32[128,4096]{1,0:T(8,128)}, f32[128,4096]{1,0:T(8,128)}, bf16[128,16384]{1,0:T(8,128)(2,1)}, f32[512,4096]{1,0:T(8,128)}) custom-call(f32[16,128,256]{2,1,0:T(8,128)S(1)} %get-tuple-element.10.master, f32[16,128,256]{2,1,0:T(8,128)S(1)} %get-tuple-element.11.moment, ...), custom_call_target="tpu_custom_call" | custom-call | tf_op jit(solution)/shard_map/pallas_call | solution.py:659
